TPU v7x, 512 devices: a whole 4x8x8 slice. The times are simulated.
512 devices in a mesh: member: 64 (over z, x, y_lo), tensor: 8 (over y_hi, core).
Axes of the slice: x: 4, y: 8 (y_hi: 4, y_lo: 2; y = y_hi * 2 + y_lo), z: 8, core: 2. Of those that a mesh axis runs over, the one named last changes fastest.
Arguments:
- tokens: bfloat16 [3072, 5120], P('member', 'tensor'), may hold values from -6 to 6
- up_weight: bfloat16 [5120, 27648], P('tensor', 'member'), may hold values from -0.078125 to 0.078125
- left_factors: bfloat16 [768, 5120], P('member', 'tensor'), may hold values from -6 to 6
- right_factors: bfloat16 [768, 27648], P('tensor', 'member'), may hold values from -6 to 6
- fitness: float32 [192], replicated, may hold values from -0.6 to 0.6
Outputs:
- hidden: bfloat16 [3072, 27648], P('tensor', 'member')
- gradient: bfloat16 [5120, 27648], P('tensor', 'member')
All inputs are finite; a program needn't handle non-finite values.
Results may differ from a plain program's by a relative error of at most 0.014.
Values may be sent and summed in bfloat16 or wider, within the bound.
No kernel may reach another device: no remote copies, remote signals or barrier semaphores. Data moves between devices by JAX's collectives and lax.ppermute only.
A program may use at most 64 MiB of HBM per device.

v0:
```python
import jax
import jax.numpy as jnp
from jax import lax
from jax.sharding import Mesh
from jax.sharding import PartitionSpec as P

D = 5120
RANK = 4
MEMBER_TOKENS = 16
MEMBER = ("member_0", "member_1", "member_2")


def copy_for_each(array, axis):
    copies = jnp.broadcast_to(array, (lax.axis_size(axis), *array.shape))
    return lax.all_to_all(copies, axis, split_axis=0, concat_axis=0, tiled=True)


def joined_along(tiles, dim):
    shape = list(tiles.shape[1:])
    shape[dim] *= tiles.shape[0]
    return jnp.moveaxis(tiles, 0, dim).reshape(shape)


def collect(array, axis, dim):
    tiles = copy_for_each(array, axis)
    return joined_along(tiles, dim)


def all_blocks(array, axes, sequence):
    tiles = array
    for k in sequence:
        tiles = lax.all_gather(tiles, axes[k])
    done = sequence[::-1]
    back = [done.index(k) for k in range(len(axes))]
    tiles = tiles.transpose(*back, *range(len(axes), tiles.ndim))
    return tiles.reshape(-1, *array.shape)


def whole_of(array, axes, sequence, dim):
    return joined_along(all_blocks(array, axes, sequence), dim)


def body(tokens, up_weight, left_factors, right_factors, fitness):
    noise_scale = 0.25 * D ** (-0.5)
    mixing = noise_scale * RANK ** (-0.5)
    block_span_width = tokens.shape[1]
    column_width = up_weight.shape[1]
    right_all = collect(right_factors, "tensor", 0)
    members = right_all.shape[0] // RANK
    local_count = tokens.shape[0] // MEMBER_TOKENS
    local_proj = jnp.einsum(
        "uzg,uig->uzi",
        tokens.reshape(local_count, MEMBER_TOKENS, block_span_width),
        left_factors.reshape(local_count, RANK, block_span_width),
        preferred_element_type=jnp.float32,
    ).astype(jnp.bfloat16)
    all_tokens, up_projection = (
        whole_of(tokens, MEMBER, (2, 0, 1), 0),
        whole_of(local_proj, MEMBER, (2, 0, 1), 0),
    )
    left_all = collect(left_factors, MEMBER, 0)
    right_factor_grouped = right_all.reshape(members, RANK, column_width)
    base_block = jnp.dot(all_tokens, up_weight, preferred_element_type=jnp.float32)
    corr_block = jnp.einsum(
        "djt,dty->djy", up_projection, right_factor_grouped, preferred_element_type=jnp.float32
    ).reshape(base_block.shape)
    summed = lax.psum_scatter(
        (base_block + mixing * corr_block).astype(jnp.bfloat16),
        "tensor",
        scatter_dimension=0,
        tiled=True,
    )
    fit_rows = jnp.repeat(fitness, RANK)
    weighted = (fit_rows[:, None] * left_all.astype(jnp.float32)).astype(jnp.bfloat16)
    gradient = jnp.einsum("kd,kf->df", weighted, right_all, preferred_element_type=jnp.float32)
    gradient = gradient * (1.0 / (members * noise_scale * RANK**0.5))
    return (summed, gradient.astype(jnp.bfloat16))


def solution(mesh):
    finer = Mesh(
        mesh.devices.reshape(8, 4, 2, mesh.shape["tensor"]),
        ("member_0", "member_1", "member_2", "tensor"),
    )
    return jax.shard_map(
        body,
        mesh=finer,
        in_specs=(
            P(MEMBER, "tensor"),
            P("tensor", MEMBER),
            P(MEMBER, "tensor"),
            P("tensor", MEMBER),
            P(),
        ),
        out_specs=(P("tensor", MEMBER), P("tensor", MEMBER)),
        check_vma=False,
    )
```

profile of v0, /device:TPU:6, one launch (start us, length us, event | category | flops | bytes accessed | tf_op | source)
XLA Modules:
  0.0 194.2 jit_solution(5574932140828432322)
XLA Ops:
  7.2 0.0 copy-start
  7.2 0.0 copy-start.4
  7.2 0.0 copy-start.3
  7.2 0.0 all-gather.8.cloned.1.call-start
  7.2 5.2 %all-gather = bf16[96,640]{1,0:T(8,128)(2,1)S(1)} all-gather(bf16[48,640]{1,0:T(8,128)(2,1)} %param.5), channel_id=2, replica_groups=mesh['member_0'=8,'member_1'=4,'member_2'=2,'tensor'=8] {'member_2'}, dimensions={0}, use_global_device_ids=true | all-gather | bytes 184320 | tf_op jit(solution)/shard_map/all_gather | solution.py:32
  12.5 35.3 %all-gather.1 = bf16[16,48,640]{2,1,0:T(8,128)(2,1)} all-gather(bf16[2,48,640]{2,1,0:T(8,128)(2,1)S(1)} %bitcast.35), channel_id=3, replica_groups=mesh['member_0'=8,'member_1'=4,'member_2'=2,'tensor'=8] {'member_0'}, dimensions={0}, use_global_device_ids=true | all-gather | bytes 1105920 | tf_op jit(solution)/shard_map/all_gather | solution.py:32
  47.7 0.0 all-gather.8.cloned.1.call-update
  47.8 1.9 broadcast_in_dim.13
  49.6 7.1 %all-to-all-start = ((bf16[8,96,432]{2,1,0:T(8,128)(2,1)}), bf16[8,96,432]{2,1,0:T(8,128)(2,1)S(1)}, u32[]{:S(2)}, u32[]{:S(2)}) async-start(bf16[8,96,432]{2,1,0:T(8,128)(2,1)} %broadcast_in_dim.13), calls=%async_computation | async-start | bytes 1572864 | tf_op jit(solution)/shard_map/all_to_all | solution.py:15
  56.7 0.0 reduce-scatter.4.cloned.1.call-start
  56.8 0.0 copy-done.3
  56.8 0.0 copy-done.4
  56.8 0.1 convolution_convert_fusion
  56.9 16.0 %all-gather.3 = bf16[6,16,4]{1,2,0:T(4,128)(2,1)S(1)} all-gather(bf16[3,16,4]{1,2,0:T(4,128)(2,1)S(1)} %convolution_convert_fusion), channel_id=5, replica_groups=mesh['member_0'=8,'member_1'=4,'member_2'=2,'tensor'=8] {'member_2'}, dimensions={0}, use_global_device_ids=true | all-gather | bytes 1152 | tf_op jit(solution)/shard_map/all_gather | solution.py:32
  73.0 24.8 %all-gather.4 = bf16[16,3,16,4]{2,3,1,0:T(4,128)(2,1)S(1)} all-gather(bf16[2,3,16,4]{2,3,1,0:T(4,128)(2,1)S(1)} %bitcast.38), channel_id=6, replica_groups=mesh['member_0'=8,'member_1'=4,'member_2'=2,'tensor'=8] {'member_0'}, dimensions={0}, use_global_device_ids=true | all-gather | bytes 6912 | tf_op jit(solution)/shard_map/all_gather | solution.py:32
  97.8 12.1 %all-gather.5 = bf16[32,2,3,16,4]{3,1,0,4,2:T(2,128)(2,1)S(1)} all-gather(bf16[8,2,3,16,4]{3,1,0,4,2:T(2,128)(2,1)S(1)} %bitcast.36), channel_id=7, replica_groups=mesh['member_0'=8,'member_1'=4,'member_2'=2,'tensor'=8] {'member_1'}, dimensions={0}, use_global_device_ids=true | all-gather | bytes 30720 | tf_op jit(solution)/shard_map/all_gather | solution.py:32
  110.0 0.1 copy.22
  110.1 0.0 all-to-all-done
  110.1 0.0 copy-start.2
  110.1 0.2 reshape_reshape.11
  110.3 3.3 %broadcast_multiply_fusion = f32[192,16,432]{2,1,0:T(8,128)} fusion(bf16[192,16,4]{1,2,0:T(4,128)(2,1)S(1)} %bitcast.34, bf16[192,4,432]{2,1,0:T(4,128)(2,1)S(1)} %reshape_reshape.11), kind=kOutput, calls=%fused_computation.1 | convolution fusion | flops 11943936 | bytes 5996544 | tf_op jit(solution)/shard_map/djt,dty->djy/dot_general | solution.py:64
  113.6 0.0 copy-done.2
  113.6 6.3 %copy.23 = f32[3072,432]{0,1:T(8,128)} copy(f32[3072,432]{1,0:T(8,128)} %bitcast.28) | data formatting | bytes 10616832 | tf_op jit(solution)/shard_map/mul | solution.py:68
  119.9 0.0 all-gather.8.cloned.1.call-done
  119.9 0.0 copy-start.1
  119.9 2.7 %copy.19 = bf16[8,4,2,48,640]{4,3,2,1,0:T(8,128)(2,1)S(1)} copy(bf16[8,4,2,48,640]{4,3,2,0,1:T(8,128)(2,1)} %bitcast.29) | data formatting | bytes 7864320 | tf_op jit(solution)/shard_map/transpose | solution.py:35
  122.6 0.0 copy-done
  122.6 1.0 copy-done.1
  123.6 2.3 %add_convert_fusion = bf16[3072,432]{0,1:T(8,128)(2,1)S(1)} fusion(f32[3072,432]{0,1:T(8,128)S(1)} %copy-done.1, bf16[3072,640]{1,0:T(8,128)(2,1)S(1)} %bitcast.30, bf16[640,432]{0,1:T(8,128)(2,1)S(1)} %copy-done), kind=kOutput, calls=%fused_computation | convolution fusion | flops 1701347328 | bytes 12447744 | tf_op jit(solution)/shard_map/dot_general | solution.py:63
  125.9 2.8 %copy.26 = bf16[3072,432]{1,0:T(8,128)(2,1)} copy(bf16[3072,432]{0,1:T(8,128)(2,1)S(1)} %add_convert_fusion) | data formatting | bytes 5308416
  128.7 0.0 copy-start.5
  128.7 0.0 reduce-scatter.4.cloned.1.call-update
  128.7 1.2 broadcast_in_dim.17
  129.9 8.7 %all-to-all-start.1 = ((bf16[64,12,640]{2,1,0:T(8,128)(2,1)}), bf16[64,12,640]{2,1,0:T(8,128)(2,1)S(1)}, u32[]{:S(2)}, u32[]{:S(2)}) async-start(bf16[64,12,640]{2,1,0:T(8,128)(2,1)} %broadcast_in_dim.17), calls=%async_computation.1 | async-start | bytes 2621440 | tf_op jit(solution)/shard_map/all_to_all | solution.py:15
  138.6 0.0 copy-done.5
  138.6 0.1 broadcast_in_dim.14
  138.7 0.1 copy.24
  138.8 0.1 copy.25
  138.9 27.0 %all-to-all-done.1 = bf16[64,12,640]{2,1,0:T(8,128)(2,1)S(1)} async-done(((bf16[64,12,640]{2,1,0:T(8,128)(2,1)}), bf16[64,12,640]{2,1,0:T(8,128)(2,1)S(1)}, u32[]{:S(2)}, u32[]{:S(2)}) %all-to-all-start.1) | async-done | bytes 983072 | tf_op jit(solution)/shard_map/all_to_all | solution.py:15
  166.0 0.3 multiply_convert_fusion
  166.3 0.3 convert_element_type.23
  166.5 2.7 %fusion = bf16[640,432]{0,1:T(8,128)(2,1)} fusion(bf16[768,640]{1,0:T(8,128)(2,1)S(1)} %convert_element_type.23, bf16[768,432]{1,0:T(8,128)(2,1)} %bitcast.32), kind=kOutput, calls=%fused_computation.4 | convolution fusion | flops 425226240 | bytes 2199552 | tf_op jit(solution)/shard_map/kd,kf->df/dot_general | solution.py:75
  169.2 16.3 %reduce-scatter.4.cloned.1.call-done = bf16[384,432]{1,0:T(8,128)(2,1)} async-done(((bf16[3072,432]{1,0:T(8,128)(2,1)}), bf16[384,432]{1,0:T(8,128)(2,1)}) %reduce-scatter.4.cloned.1.call-update) | async-done | bytes 331792
  185.5 1.9 copy.27
  (5 shorter events, 0.1 us)
Async XLA Ops:
  7.2 115.4 %copy-start = (bf16[640,432]{0,1:T(8,128)(2,1)S(1)}, bf16[640,432]{0,1:T(8,128)(2,1)}, u32[]{:S(2)}) copy-start(bf16[640,432]{0,1:T(8,128)(2,1)} %param.6) | copy-start | bytes 1658884
  7.2 49.6 %copy-start.4 = (bf16[48,640]{1,0:T(8,128)(2,1)S(1)}, bf16[48,640]{1,0:T(8,128)(2,1)}, u32[]{:S(2)}) copy-start(bf16[48,640]{1,0:T(8,128)(2,1)} %param.5) | copy-start | bytes 184324
  7.2 49.6 %copy-start.3 = (bf16[12,640]{1,0:T(8,128)(2,1)S(1)}, bf16[12,640]{1,0:T(8,128)(2,1)}, u32[]{:S(2)}) copy-start(bf16[12,640]{1,0:T(8,128)(2,1)} %param.7) | copy-start | bytes 46084
  7.2 112.7 %all-gather.8.cloned.1.call-start = ((), (), s32[]{:S(2)}) async-start(), calls=%async_computation.3 | async-start | bytes 4915200 | tf_op jit(solution)/shard_map/all_gather | solution.py:32
  49.6 60.5 %all-to-all-start = ((bf16[8,96,432]{2,1,0:T(8,128)(2,1)}), bf16[8,96,432]{2,1,0:T(8,128)(2,1)S(1)}, u32[]{:S(2)}, u32[]{:S(2)}) async-start(bf16[8,96,432]{2,1,0:T(8,128)(2,1)} %broadcast_in_dim.13), calls=%async_computation | async-start | bytes 1572864 | tf_op jit(solution)/shard_map/all_to_all | solution.py:15
  56.7 128.8 %reduce-scatter.4.cloned.1.call-start = ((), (), s32[]{:S(2)}) async-start(), calls=%async_computation.4 | async-start | bytes 3538944
  110.1 3.5 %copy-start.2 = (bf16[8,96,432]{2,1,0:T(8,128)(2,1)}, bf16[8,96,432]{2,1,0:T(8,128)(2,1)S(1)}, u32[]{:S(2)}) copy-start(bf16[8,96,432]{2,1,0:T(8,128)(2,1)S(1)} %all-to-all-done) | copy-start | bytes 1990660
  119.9 3.7 %copy-start.1 = (f32[3072,432]{0,1:T(8,128)S(1)}, f32[3072,432]{0,1:T(8,128)}, u32[]{:S(2)}) copy-start(f32[3072,432]{0,1:T(8,128)} %copy.23) | copy-start | bytes 15925252
  128.7 9.9 %copy-start.5 = (f32[192]{0:T(256)S(1)}, f32[192]{0:T(256)}, u32[]{:S(2)}) copy-start(f32[192]{0:T(256)} %param.9) | copy-start | bytes 2308
  129.9 36.1 %all-to-all-start.1 = ((bf16[64,12,640]{2,1,0:T(8,128)(2,1)}), bf16[64,12,640]{2,1,0:T(8,128)(2,1)S(1)}, u32[]{:S(2)}, u32[]{:S(2)}) async-start(bf16[64,12,640]{2,1,0:T(8,128)(2,1)} %broadcast_in_dim.17), calls=%async_computation.1 | async-start | bytes 2621440 | tf_op jit(solution)/shard_map/all_to_all | solution.py:15
Sparse Core Ops, SparseCore 0:
  47.9 47.4 all-gather.7
  128.8 56.6 reduce-scatter.3
where the time goes:
time: 195 us; the launch traced here: 194 us
  blocking collectives  93.5 us (48%)
  waiting for transfers between devices  43.3 us (22%)
  local copies, waits for them, and re-layouts  18.6 us (10%)
  starting transfers between devices  15.9 us (8%)
  between operations  14.2 us (7%)
  matrix products  8.42 us (4%)
    all_gather x5, blocking collectives, all_blocks(): tiles = lax.all_gather(tiles, axes[k])  93.5 us
    all_to_all x2, waiting for transfers between devices, copy_for_each(): return lax.all_to_all(copies, axis, split_axis=0, concat_axis=0, tiled=True)  27 us
    unnamed x3, waiting for transfers between devices  16.3 us
    all_to_all x2, starting transfers between devices, copy_for_each(): return lax.all_to_all(copies, axis, split_axis=0, concat_axis=0, tiled=True)  15.8 us
    mul x1, local copies, waits for them, and re-layouts, body(): mixing * corr_block  6.27 us
    unnamed x14, local copies, waits for them, and re-layouts  5.69 us
  transfers between devices with their start and end apart: 4, of which 2 were waited for; matrix products, arithmetic and copies ran while one was open for 9% of the time, Pallas kernels for 0%

commit v1 on v0

v1 whole, which is shorter than its diff:
```python
import itertools

import jax
import jax.numpy as jnp
from jax import lax
from jax.sharding import Mesh
from jax.sharding import PartitionSpec as P

D = 5120
RANK = 4
MEMBER_TOKENS = 16
POPULATION = 192
MEMBER = ("z", "x", "lo")
TENSOR = ("hi", "core")
SIGMA = 0.25 * D**-0.5
MIXING = SIGMA * RANK**-0.5
GRADIENT_SCALE = 1.0 / (POPULATION * SIGMA * RANK**0.5)


def shifted(array, axis, step):
    size = lax.axis_size(axis)
    return lax.ppermute(array, axis, [(k, (k + step) % size) for k in range(size)])


def gathered(array, axes):
    copies = jnp.broadcast_to(array, (lax.axis_size(axes), *array.shape))
    return lax.all_to_all(copies, axes, split_axis=0, concat_axis=0, tiled=True)


def wrapped(stack, start, sign=1):
    count = stack.shape[0]
    order = (start + sign * jnp.arange(count)) % count
    return jnp.take(stack, order, axis=0, mode="clip")


def dot_t(a, b):
    return lax.dot_general(a, b, (((1,), (1,)), ((), ())), preferred_element_type=jnp.float32)


def body(tokens, up_weight, left_factors, right_factors, fitness):
    f32, bf16 = jnp.float32, jnp.bfloat16
    hi, core, x = lax.axis_index("hi"), lax.axis_index("core"), lax.axis_index("x")
    rows, features = tokens.shape
    factors = left_factors.shape[0]
    columns = up_weight.shape[1]
    n_x, n_hi, n_z, n_lo = (lax.axis_size(a) for a in ("x", "hi", "z", "lo"))
    wide = -(-(n_x * columns + RANK) // 128) * 128

    weight = up_weight.T
    weight_after = shifted(weight, "x", -1)
    weight_before = shifted(weight, "x", 1)
    mine = jnp.concatenate([tokens, left_factors, jnp.zeros((4, features), bf16)], 0)
    near = gathered(mine, ("z", "lo"))
    half = columns // 2
    weight_far = jnp.concatenate(
        [
            shifted(weight_before[:half], "x", 1),
            shifted(weight_after[half:], "x", -1),
        ],
        0,
    )
    right_all = gathered(right_factors, TENSOR)
    near, right_all = lax.optimization_barrier((near, right_all))
    near_left = near[:, rows : rows + factors]
    weights = jnp.concatenate(
        [weight, weight_after, weight_far, weight_before, jnp.zeros((wide - n_x * columns, features), bf16)], 0
    )

    block = n_lo * rows
    token_blocks = near[:, :rows].reshape(n_hi, 2, block, features)
    left_blocks = near_left.reshape(n_hi, 2, n_lo * factors, features)
    row = lax.broadcasted_iota(jnp.int32, (n_hi * block, n_hi * n_lo * factors), 0)
    col = lax.broadcasted_iota(jnp.int32, (n_hi * block, n_hi * n_lo * factors), 1)
    same = row // MEMBER_TOKENS == col // RANK
    k = lax.broadcasted_iota(jnp.int32, (wide, n_hi * n_lo * factors), 1)
    c = lax.broadcasted_iota(jnp.int32, (wide, n_hi * n_lo * factors), 0)
    place = (c == n_x * columns + k % RANK).astype(bf16)

    def partial(side):
        some = wrapped(lax.dynamic_index_in_dim(token_blocks, side, 1, False), hi)
        lefts = wrapped(lax.dynamic_index_in_dim(left_blocks, side, 1, False), hi)
        some = some.reshape(n_hi * block, features)
        lefts = lefts.reshape(-1, features)
        projection = jnp.where(same, dot_t(some, lefts), 0.0).astype(bf16)
        return (dot_t(some, weights) + dot_t(projection, place)).reshape(n_hi, block, wide)

    sent = partial(1 - core).astype(bf16)
    other = shifted(sent, "core", 1)
    both = (partial(core) + other.astype(f32)).astype(bf16)
    cut = block // 2
    via_after = shifted(both[2, :cut], "hi", 1)
    via_before = shifted(both[2, cut:], "hi", -1)
    to_after = jnp.concatenate(
        [(both[1, :cut].astype(f32) + via_after.astype(f32)).astype(bf16), both[1, cut:]], 0
    )
    to_before = jnp.concatenate(
        [both[3, :cut], (both[3, cut:].astype(f32) + via_before.astype(f32)).astype(bf16)], 0
    )
    from_before = shifted(to_after, "hi", 1)
    from_after = shifted(to_before, "hi", -1)
    total = both[0].astype(f32) + from_before.astype(f32) + from_after.astype(f32)
    total = total.astype(bf16)

    pieces = []
    for j in range(n_x):
        piece = jnp.concatenate(
            [total[:, j * columns : (j + 1) * columns], total[:, n_x * columns : n_x * columns + RANK]], 1
        )
        pieces.append(shifted(piece, "x", j) if j else piece)
    whole = wrapped(jnp.stack(pieces), x, -1).reshape(n_x * block, columns + RANK)
    own = right_factors.shape[0]
    row = lax.broadcasted_iota(jnp.int32, (n_x * block, own), 0)
    col = lax.broadcasted_iota(jnp.int32, (n_x * block, own), 1)
    tiled = jnp.tile(whole[:, columns:], (1, own // RANK))
    spread = jnp.where(row // MEMBER_TOKENS == col // RANK, tiled, 0)
    correction = jnp.dot(spread, right_factors, preferred_element_type=f32)
    hidden = (whole[:, :columns].astype(f32) + MIXING * correction).astype(bf16)

    left_all = gathered(near_left, "x")
    left_all = left_all.reshape(n_x, n_z, n_lo * factors, features).transpose(1, 0, 2, 3)
    left_all = left_all.reshape(-1, features)
    fit = jnp.repeat(fitness, RANK)
    weighted = (fit[:, None] * left_all.astype(f32)).astype(bf16)
    right_all = right_all.reshape(-1, columns)
    gradient = jnp.einsum("kd,kf->df", weighted, right_all, preferred_element_type=f32)
    return hidden, (gradient * GRADIENT_SCALE).astype(bf16)


def solution(mesh):
    finer = Mesh(mesh.devices.reshape(8, 4, 2, 4, 2), MEMBER + TENSOR)
    return jax.shard_map(
        body,
        mesh=finer,
        in_specs=(P(MEMBER, TENSOR), P(TENSOR, MEMBER), P(MEMBER, TENSOR), P(TENSOR, MEMBER), P()),
        out_specs=(P(TENSOR, MEMBER), P(TENSOR, MEMBER)),
        check_vma=False,
    )
```

time: 195 us -> 163 us (0.84)
  blocking collectives: 93.5 us -> 0 us
  starting transfers between devices: 15.9 us -> 59.6 us
  waiting for transfers between devices: 43.3 us -> 58.4 us
  between operations: 14.2 us -> 1.09 us
  matrix products: 8.42 us -> 16 us
  other arithmetic: 0.29 us -> 5.46 us
  local copies, waits for them, and re-layouts: 18.6 us -> 21.1 us
    all_gather x5 -> x0, blocking collectives: 93.5 us -> none  [all_blocks(): tiles = lax.all_gather(tiles, axes[k])]
    ppermute x0 -> x12, starting transfers between devices: none -> 37.2 us  [shifted(): lax.ppermute(array, axis, [(k, (k + step) % size) for k in range(size)])]
    ppermute x0 -> x12, waiting for transfers between devices: none -> 32.4 us  [shifted(): lax.ppermute(array, axis, [(k, (k + step) % size) for k in range(size)])]
    unnamed x3 -> x0, waiting for transfers between devices: 16.3 us -> none
    dot_general x4 -> x6, matrix products: 8.42 us -> 16 us  [the longest x4 13.3 us: dot_t(): lax.dot_general(a, b, (((1,), (1,)), ((), ())), preferred_element_type=jn...]
    all_to_all x2 -> x3, starting transfers between devices: 15.8 us -> 22.5 us  [gathered(): return lax.all_to_all(copies, axes, split_axis=0, concat_axis=0, tiled=True)]
    mul x1 -> x0, local copies, waits for them, and re-layouts: 6.27 us -> none  [body(): mixing * corr_block]
    slice x0 -> x9, local copies, waits for them, and re-layouts: none -> 4.9 us  [the longest x2 1.77 us: body(): near_left = near[:, rows:rows + factors]]
  transfers between devices with their start and end apart: 4 -> 15, of which waited for: 2 -> 11; matrix products, arithmetic and copies ran while one was open for 9% -> 11% of each run, Pallas kernels for 0% -> 0%
where the time goes in v1:
time: 163 us; the launch traced here: 162 us
  starting transfers between devices  59.6 us (37%)
  waiting for transfers between devices  58.4 us (36%)
  local copies, waits for them, and re-layouts  21.1 us (13%)
  matrix products  16 us (10%)
  other arithmetic  5.46 us (3%)
    ppermute x12, starting transfers between devices, shifted(): lax.ppermute(array, axis, [(k, (k + step) % size) for k in range(size)])  37.2 us
    ppermute x12, waiting for transfers between devices, shifted(): lax.ppermute(array, axis, [(k, (k + step) % size) for k in range(size)])  32.4 us
    all_to_all x3, waiting for transfers between devices, gathered(): return lax.all_to_all(copies, axes, split_axis=0, concat_axis=0, tiled=True)  26 us
    all_to_all x3, starting transfers between devices, gathered(): return lax.all_to_all(copies, axes, split_axis=0, concat_axis=0, tiled=True)  22.5 us
    dot_general x4, matrix products, dot_t(): lax.dot_general(a, b, (((1,), (1,)), ((), ())), preferred_element_type=jn...  13.3 us
    broadcast_in_dim x3, local copies, waits for them, and re-layouts, gathered(): copies = jnp.broadcast_to(array, (lax.axis_size(axes), *array.shape))  4.22 us
    gather x5, local copies, waits for them, and re-layouts, wrapped(): return jnp.take(stack, order, axis=0, mode='clip')  4.02 us
    unnamed x24, local copies, waits for them, and re-layouts  3.49 us
  transfers between devices with their start and end apart: 15, of which 11 were waited for; matrix products, arithmetic and copies ran while one was open for 11% of the time, Pallas kernels for 0%

profile of v1, /device:TPU:6, one launch (start us, length us, event | category | flops | bytes accessed | tf_op | source)
XLA Modules:
  0.0 161.6 jit_solution(6990229369138561674)
XLA Ops:
  0.6 1.9 %broadcast_in_dim.41 = bf16[8,96,432]{2,1,0:T(8,128)(2,1)} broadcast(bf16[96,432]{1,0:T(8,128)(2,1)} %param.8), dimensions={1,2} | broadcast | bytes 746496 | tf_op jit(solution)/shard_map/broadcast_in_dim | solution.py:26
  2.5 7.1 %all-to-all-start.1 = ((bf16[8,96,432]{2,1,0:T(8,128)(2,1)}), bf16[8,96,432]{2,1,0:T(8,128)(2,1)S(1)}, u32[]{:S(2)}, u32[]{:S(2)}) async-start(bf16[8,96,432]{2,1,0:T(8,128)(2,1)} %broadcast_in_dim.41), calls=%async_computation.1 | async-start | bytes 1572864 | tf_op jit(solution)/shard_map/all_to_all | solution.py:27
  9.8 23.1 %all-to-all-done.1 = bf16[8,96,432]{2,1,0:T(8,128)(2,1)S(1)} async-done(((bf16[8,96,432]{2,1,0:T(8,128)(2,1)}), bf16[8,96,432]{2,1,0:T(8,128)(2,1)S(1)}, u32[]{:S(2)}, u32[]{:S(2)}) %all-to-all-start.1) | async-done | bytes 663584 | tf_op jit(solution)/shard_map/all_to_all | solution.py:27
  32.9 1.3 broadcast_in_dim.40
  34.2 10.5 %all-to-all-start = ((bf16[16,64,640]{2,1,0:T(8,128)(2,1)}), bf16[16,64,640]{2,1,0:T(8,128)(2,1)}, u32[]{:S(2)}, u32[]{:S(2)}) async-start(bf16[16,64,640]{2,1,0:T(8,128)(2,1)} %broadcast_in_dim.40), calls=%async_computation | async-start | bytes 2621440 | tf_op jit(solution)/shard_map/all_to_all | solution.py:27
  44.7 2.4 %collective-permute-start.1 = (bf16[432,640]{1,0:T(8,128)(2,1)}, bf16[432,640]{1,0:T(8,128)(2,1)S(1)}, u32[]{:S(2)}, u32[]{:S(2)}) collective-permute-start(bf16[432,640]{1,0:T(8,128)(2,1)} %bitcast.4), channel_id=1, source_target_pairs={{0,16},{16,32},{32,48},{48,0},{1,17},{17,33},{33,49},{49,1},{2,18}... | collective-permute-start | bytes 1658888 | tf_op jit(solution)/shard_map/ppermute | solution.py:22
  47.1 3.5 %collective-permute-start = (bf16[432,640]{1,0:T(8,128)(2,1)}, bf16[432,640]{1,0:T(8,128)(2,1)S(1)}, u32[]{:S(2)}, u32[]{:S(2)}) collective-permute-start(bf16[432,640]{1,0:T(8,128)(2,1)} %bitcast.4), channel_id=1, source_target_pairs={{0,48},{16,0},{32,16},{48,32},{1,49},{17,1},{33,17},{49,33},{2,50}... | collective-permute-start | bytes 1658888 | tf_op jit(solution)/shard_map/ppermute | solution.py:22
  51.2 1.1 constant_dynamic-update-slice_fusion.4
  52.3 7.0 %collective-permute-done.1 = bf16[432,640]{1,0:T(8,128)(2,1)S(1)} collective-permute-done((bf16[432,640]{1,0:T(8,128)(2,1)}, bf16[432,640]{1,0:T(8,128)(2,1)S(1)}, u32[]{:S(2)}, u32[]{:S(2)}) %collective-permute-start.1) | collective-permute-done | bytes 552992 | tf_op jit(solution)/shard_map/ppermute | solution.py:22
  59.3 0.7 slice.83
  60.0 3.6 %collective-permute-start.2 = (bf16[216,640]{1,0:T(8,128)(2,1)}, bf16[216,640]{1,0:T(8,128)(2,1)}, u32[]{:S(2)}, u32[]{:S(2)}) collective-permute-start(bf16[216,640]{1,0:T(8,128)(2,1)} %slice.83), channel_id=1, source_target_pairs={{0,16},{16,32},{32,48},{48,0},{1,17},{17,33},{33,49},{49,1},{2,18}... | collective-permute-start | bytes 829448 | tf_op jit(solution)/shard_map/ppermute | solution.py:22
  64.1 0.7 slice.84
  64.8 2.2 %collective-permute-start.3 = (bf16[216,640]{1,0:T(8,128)(2,1)}, bf16[216,640]{1,0:T(8,128)(2,1)}, u32[]{:S(2)}, u32[]{:S(2)}) collective-permute-start(bf16[216,640]{1,0:T(8,128)(2,1)} %slice.84), channel_id=1, source_target_pairs={{0,48},{16,0},{32,16},{48,32},{1,49},{17,1},{33,17},{49,33},{2,50}... | collective-permute-start | bytes 829448 | tf_op jit(solution)/shard_map/ppermute | solution.py:22
  67.2 1.6 collective-permute-done.2
  68.7 1.0 constant_dynamic-update-slice_fusion.2
  69.7 5.0 %collective-permute-done.3 = bf16[216,640]{1,0:T(8,128)(2,1)} collective-permute-done((bf16[216,640]{1,0:T(8,128)(2,1)}, bf16[216,640]{1,0:T(8,128)(2,1)}, u32[]{:S(2)}, u32[]{:S(2)}) %collective-permute-start.3) | collective-permute-done | bytes 276512 | tf_op jit(solution)/shard_map/ppermute | solution.py:22
  74.7 1.0 constant_dynamic-update-slice_fusion.1
  76.5 1.7 %slice.59 = bf16[16,12,640]{2,1,0:T(8,128)(2,1)} slice(bf16[16,64,640]{2,1,0:T(8,128)(2,1)} %all-to-all-done), slice={[0:16], [48:60], [0:640]} | slice | bytes 491520 | tf_op jit(solution)/shard_map/slice | solution.py:64
  78.2 1.3 slice.56
  79.5 1.0 reshape.141
  80.5 1.1 dynamic-slice_bitcast_fusion
  81.6 0.7 dynamic-slice_bitcast_fusion.2
  82.3 1.7 %gather_fusion.2 = bf16[4,96,640]{2,1,0:T(8,128)(2,1)S(1)} fusion(bf16[4,96,640]{2,1,0:T(8,128)(2,1)} %get-tuple-element.12, s32[1024]{0:T(1024)S(1)} %pad_clamp_fusion.1), kind=kCustom, calls=%fused_computation.2 | custom fusion | bytes 983056 | tf_op jit(solution)/shard_map/jit(_take)/gather | solution.py:33
  84.5 3.0 %fusion.6 = f32[384,1792]{1,0:T(8,128)} fusion(bf16[384,640]{1,0:T(8,128)(2,1)S(1)} %bitcast.74, bf16[96,640]{1,0:T(8,128)(2,1)S(1)} %bitcast.82, s32[96]{0:T(128)} %get-tuple-element.27, s32[96]{0:T(128)S(1)} %get-tuple-element.28, pred[96]{0:T(512)(128)(4,1)} %get-tuple-element.22, s32[96]{0:T(128)S(1)} %get-tuple-element.26, ...), kind=kOutput, calls=%fused_computation.19 | convolution fusion | flops 180006912 | bytes 3372096 | tf_op jit(solution)/shard_map/dot_general | solution.py:37
  87.6 4.2 %fusion = bf16[384,1792]{1,0:T(8,128)(2,1)} fusion(f32[384,1792]{1,0:T(8,128)} %fusion.6, bf16[384,640]{1,0:T(8,128)(2,1)S(1)} %bitcast.75, bf16[1792,640]{1,0:T(8,128)(2,1)S(1)} %broadcast_dynamic-update-slice_fusion), kind=kOutput, calls=%fused_computation.7 | convolution fusion | flops 882180096 | bytes 6914048 | tf_op jit(solution)/shard_map/dot_general | solution.py:37
  91.8 1.9 %collective-permute-start.4 = (bf16[4,96,1792]{2,1,0:T(8,128)(2,1)}, bf16[4,96,1792]{2,1,0:T(8,128)(2,1)}, u32[]{:S(2)}, u32[]{:S(2)}) collective-permute-start(bf16[4,96,1792]{2,1,0:T(8,128)(2,1)} %bitcast.12), channel_id=1, source_target_pairs={{0,1},{1,0},{2,3},{3,2},{4,5},{5,4},{6,7},{7,6},{8,9},{9,8},{10,11... | collective-permute-start | bytes 4128776 | tf_op jit(solution)/shard_map/ppermute | solution.py:22
  94.3 0.6 gather_fusion
  94.9 3.0 %fusion.7 = f32[384,1792]{1,0:T(8,128)} fusion(bf16[384,640]{1,0:T(8,128)(2,1)S(1)} %bitcast.72, bf16[96,640]{1,0:T(8,128)(2,1)S(1)} %bitcast.81, s32[96]{0:T(128)} %get-tuple-element.27, s32[96]{0:T(128)S(1)} %get-tuple-element.28, pred[96]{0:T(512)(128)(4,1)} %get-tuple-element.22, s32[96]{0:T(128)S(1)} %get-tuple-element.26, ...), kind=kOutput, calls=%fused_computation.20 | convolution fusion | flops 180006912 | bytes 3372096 | tf_op jit(solution)/shard_map/dot_general | solution.py:37
  98.0 3.1 %convolution_add_fusion.1 = f32[384,1792]{1,0:T(8,128)S(1)} fusion(f32[384,1792]{1,0:T(8,128)} %fusion.7, bf16[384,640]{1,0:T(8,128)(2,1)S(1)} %bitcast.73, bf16[1792,640]{1,0:T(8,128)(2,1)S(1)} %broadcast_dynamic-update-slice_fusion), kind=kOutput, calls=%fused_computation.6 | convolution fusion | flops 881491968 | bytes 8290304 | tf_op jit(solution)/shard_map/dot_general | solution.py:37
  101.1 1.7 %add_convert_fusion = bf16[4,96,1792]{2,1,0:T(8,128)(2,1)S(1)} fusion(f32[4,96,1792]{2,1,0:T(8,128)S(1)} %bitcast.70, bf16[4,96,1792]{2,1,0:T(8,128)(2,1)} %collective-permute-done.4), kind=kLoop, calls=%fused_computation.8 | loop fusion | flops 2064384 | bytes 5505024 | tf_op jit(solution)/shard_map/convert_element_type | solution.py:89
  102.8 4.1 %collective-permute-start.5 = (bf16[48,1792]{1,0:T(8,128)(2,1)S(1)}, bf16[48,1792]{1,0:T(8,128)(2,1)S(1)}, u32[]{:S(2)}, u32[]{:S(2)}) collective-permute-start(bf16[48,1792]{1,0:T(8,128)(2,1)S(1)} %get-tuple-element.8), channel_id=1, source_target_pairs={{0,2},{2,4},{4,6},{6,0},{1,3},{3,5},{5,7},{7,1},{8,10},{10,12},{12... | collective-permute-start | bytes 516104 | tf_op jit(solution)/shard_map/ppermute | solution.py:22
  106.9 3.9 %collective-permute-start.7 = (bf16[48,1792]{1,0:T(8,128)(2,1)S(1)}, bf16[48,1792]{1,0:T(8,128)(2,1)S(1)}, u32[]{:S(2)}, u32[]{:S(2)}) collective-permute-start(bf16[48,1792]{1,0:T(8,128)(2,1)S(1)} %get-tuple-element.9), channel_id=1, source_target_pairs={{0,6},{2,0},{4,2},{6,4},{1,7},{3,1},{5,3},{7,5},{8,14},{10,8},{12,... | collective-permute-start | bytes 516104 | tf_op jit(solution)/shard_map/ppermute | solution.py:22
  110.9 1.0 broadcast_in_dim.48
  111.9 4.9 %all-to-all-start.2 = ((bf16[4,16,12,640]{3,1,2,0:T(8,128)(2,1)}), bf16[4,16,12,640]{3,1,2,0:T(8,128)(2,1)S(1)}, u32[]{:S(2)}, u32[]{:S(2)}) async-start(bf16[4,16,12,640]{3,1,2,0:T(8,128)(2,1)} %broadcast_in_dim.48), calls=%async_computation.2 | async-start | bytes 1966080 | tf_op jit(solution)/shard_map/all_to_all | solution.py:27
  116.8 1.8 %collective-permute-done.7 = bf16[48,1792]{1,0:T(8,128)(2,1)S(1)} collective-permute-done((bf16[48,1792]{1,0:T(8,128)(2,1)S(1)}, bf16[48,1792]{1,0:T(8,128)(2,1)S(1)}, u32[]{:S(2)}, u32[]{:S(2)}) %collective-permute-start.7) | collective-permute-done | bytes 172064 | tf_op jit(solution)/shard_map/ppermute | solution.py:22
  118.8 5.1 %collective-permute-start.8 = (bf16[96,1792]{1,0:T(8,128)(2,1)S(1)}, bf16[96,1792]{1,0:T(8,128)(2,1)S(1)}, u32[]{:S(2)}, u32[]{:S(2)}) collective-permute-start(bf16[96,1792]{1,0:T(8,128)(2,1)S(1)} %pad_maximum_fusion.2), channel_id=1, source_target_pairs={{0,6},{2,0},{4,2},{6,4},{1,7},{3,1},{5,3},{7,5},{8,14},{10,8},{12,... | collective-permute-start | bytes 1032200 | tf_op jit(solution)/shard_map/ppermute | solution.py:22
  123.8 0.8 pad_maximum_fusion.1
  124.6 1.9 %collective-permute-start.6 = (bf16[96,1792]{1,0:T(8,128)(2,1)}, bf16[96,1792]{1,0:T(8,128)(2,1)}, u32[]{:S(2)}, u32[]{:S(2)}) collective-permute-start(bf16[96,1792]{1,0:T(8,128)(2,1)} %pad_maximum_fusion.1), channel_id=1, source_target_pairs={{0,2},{2,4},{4,6},{6,0},{1,3},{3,5},{5,7},{7,1},{8,10},{10,12},{12... | collective-permute-start | bytes 1032200 | tf_op jit(solution)/shard_map/ppermute | solution.py:22
  127.0 2.3 %all-to-all-done.2 = bf16[4,16,12,640]{3,1,2,0:T(8,128)(2,1)S(1)} async-done(((bf16[4,16,12,640]{3,1,2,0:T(8,128)(2,1)}), bf16[4,16,12,640]{3,1,2,0:T(8,128)(2,1)S(1)}, u32[]{:S(2)}, u32[]{:S(2)}) %all-to-all-start.2) | async-done | bytes 983072 | tf_op jit(solution)/shard_map/all_to_all | solution.py:27
  129.3 0.8 copy.29
  130.9 12.5 %collective-permute-done.6 = bf16[96,1792]{1,0:T(8,128)(2,1)} collective-permute-done((bf16[96,1792]{1,0:T(8,128)(2,1)}, bf16[96,1792]{1,0:T(8,128)(2,1)}, u32[]{:S(2)}, u32[]{:S(2)}) %collective-permute-start.6) | collective-permute-done | bytes 344096 | tf_op jit(solution)/shard_map/ppermute | solution.py:22
  143.4 1.1 fusion.9
  144.9 2.4 %collective-permute-start.9 = (bf16[96,436]{1,0:T(8,128)(2,1)S(1)}, bf16[96,436]{1,0:T(8,128)(2,1)S(1)}, u32[]{:S(2)}, u32[]{:S(2)}) collective-permute-start(bf16[96,436]{1,0:T(8,128)(2,1)S(1)} %get-tuple-element.20), channel_id=1, source_target_pairs={{0,16},{16,32},{32,48},{48,0},{1,17},{17,33},{33,49},{49,1},{2,18}... | collective-permute-start | bytes 251144 | tf_op jit(solution)/shard_map/ppermute | solution.py:22
  147.3 4.3 %collective-permute-start.10 = (bf16[96,436]{1,0:T(8,128)(2,1)S(1)}, bf16[96,436]{1,0:T(8,128)(2,1)S(1)}, u32[]{:S(2)}, u32[]{:S(2)}) collective-permute-start(bf16[96,436]{1,0:T(8,128)(2,1)S(1)} %get-tuple-element.21), channel_id=1, source_target_pairs={{0,32},{16,48},{32,0},{48,16},{1,33},{17,49},{33,1},{49,17},{2,34}... | collective-permute-start | bytes 251144 | tf_op jit(solution)/shard_map/ppermute | solution.py:22
  151.7 1.9 %collective-permute-start.11 = (bf16[96,436]{1,0:T(8,128)(2,1)S(1)}, bf16[96,436]{1,0:T(8,128)(2,1)S(1)}, u32[]{:S(2)}, u32[]{:S(2)}) collective-permute-start(bf16[96,436]{1,0:T(8,128)(2,1)S(1)} %concatenate.32), channel_id=1, source_target_pairs={{0,48},{16,0},{32,16},{48,32},{1,49},{17,1},{33,17},{49,33},{2,50}... | collective-permute-start | bytes 251144 | tf_op jit(solution)/shard_map/ppermute | solution.py:22
  153.6 1.5 fusion.1
  155.3 4.1 %collective-permute-done.11 = bf16[96,436]{1,0:T(8,128)(2,1)S(1)} collective-permute-done((bf16[96,436]{1,0:T(8,128)(2,1)S(1)}, bf16[96,436]{1,0:T(8,128)(2,1)S(1)}, u32[]{:S(2)}, u32[]{:S(2)}) %collective-permute-start.11) | collective-permute-done | bytes 83744 | tf_op jit(solution)/shard_map/ppermute | solution.py:22
  160.6 1.1 fusion.3
  (63 shorter events, 6.4 us)
Async XLA Ops:
  0.6 9.1 %copy-start.7 = (bf16[12,640]{1,0:T(8,128)(2,1)S(1)}, bf16[12,640]{1,0:T(8,128)(2,1)}, u32[]{:S(2)}) copy-start(bf16[12,640]{1,0:T(8,128)(2,1)} %param.7) | copy-start | bytes 46084
  0.6 9.1 %copy-start.6 = (bf16[48,640]{1,0:T(8,128)(2,1)S(1)}, bf16[48,640]{1,0:T(8,128)(2,1)}, u32[]{:S(2)}) copy-start(bf16[48,640]{1,0:T(8,128)(2,1)} %param.5) | copy-start | bytes 184324
  2.5 30.4 %all-to-all-start.1 = ((bf16[8,96,432]{2,1,0:T(8,128)(2,1)}), bf16[8,96,432]{2,1,0:T(8,128)(2,1)S(1)}, u32[]{:S(2)}, u32[]{:S(2)}) async-start(bf16[8,96,432]{2,1,0:T(8,128)(2,1)} %broadcast_in_dim.41), calls=%async_computation.1 | async-start | bytes 1572864 | tf_op jit(solution)/shard_map/all_to_all | solution.py:27
  32.9 18.2 %copy-start.2 = (bf16[8,96,432]{2,1,0:T(8,128)(2,1)}, bf16[8,96,432]{2,1,0:T(8,128)(2,1)S(1)}, u32[]{:S(2)}) copy-start(bf16[8,96,432]{2,1,0:T(8,128)(2,1)S(1)} %all-to-all-done.1) | copy-start | bytes 1990660
  34.2 42.2 %all-to-all-start = ((bf16[16,64,640]{2,1,0:T(8,128)(2,1)}), bf16[16,64,640]{2,1,0:T(8,128)(2,1)}, u32[]{:S(2)}, u32[]{:S(2)}) async-start(bf16[16,64,640]{2,1,0:T(8,128)(2,1)} %broadcast_in_dim.40), calls=%async_computation | async-start | bytes 2621440 | tf_op jit(solution)/shard_map/all_to_all | solution.py:27
  44.7 14.6 %collective-permute-start.1 = (bf16[432,640]{1,0:T(8,128)(2,1)}, bf16[432,640]{1,0:T(8,128)(2,1)S(1)}, u32[]{:S(2)}, u32[]{:S(2)}) collective-permute-start(bf16[432,640]{1,0:T(8,128)(2,1)} %bitcast.4), channel_id=1, source_target_pairs={{0,16},{16,32},{32,48},{48,0},{1,17},{17,33},{33,49},{49,1},{2,18}... | collective-permute-start | bytes 1658888 | tf_op jit(solution)/shard_map/ppermute | solution.py:22
  47.1 17.0 %collective-permute-start = (bf16[432,640]{1,0:T(8,128)(2,1)}, bf16[432,640]{1,0:T(8,128)(2,1)S(1)}, u32[]{:S(2)}, u32[]{:S(2)}) collective-permute-start(bf16[432,640]{1,0:T(8,128)(2,1)} %bitcast.4), channel_id=1, source_target_pairs={{0,48},{16,0},{32,16},{48,32},{1,49},{17,1},{33,17},{49,33},{2,50}... | collective-permute-start | bytes 1658888 | tf_op jit(solution)/shard_map/ppermute | solution.py:22
  60.0 8.7 %collective-permute-start.2 = (bf16[216,640]{1,0:T(8,128)(2,1)}, bf16[216,640]{1,0:T(8,128)(2,1)}, u32[]{:S(2)}, u32[]{:S(2)}) collective-permute-start(bf16[216,640]{1,0:T(8,128)(2,1)} %slice.83), channel_id=1, source_target_pairs={{0,16},{16,32},{32,48},{48,0},{1,17},{17,33},{33,49},{49,1},{2,18}... | collective-permute-start | bytes 829448 | tf_op jit(solution)/shard_map/ppermute | solution.py:22
  64.8 9.9 %collective-permute-start.3 = (bf16[216,640]{1,0:T(8,128)(2,1)}, bf16[216,640]{1,0:T(8,128)(2,1)}, u32[]{:S(2)}, u32[]{:S(2)}) collective-permute-start(bf16[216,640]{1,0:T(8,128)(2,1)} %slice.84), channel_id=1, source_target_pairs={{0,48},{16,0},{32,16},{48,32},{1,49},{17,1},{33,17},{49,33},{2,50}... | collective-permute-start | bytes 829448 | tf_op jit(solution)/shard_map/ppermute | solution.py:22
  87.6 6.1 %copy-start.4 = (bf16[4,24,640]{2,1,0:T(8,128)(2,1)S(1)}, bf16[4,24,640]{2,1,0:T(8,128)(2,1)}, u32[]{:S(2)}) copy-start(bf16[4,24,640]{2,1,0:T(8,128)(2,1)} %get-tuple-element.18) | copy-start | bytes 368644
  87.6 6.7 %copy-start.1 = (bf16[4,96,640]{2,1,0:T(8,128)(2,1)S(1)}, bf16[4,96,640]{2,1,0:T(8,128)(2,1)}, u32[]{:S(2)}) copy-start(bf16[4,96,640]{2,1,0:T(8,128)(2,1)} %get-tuple-element.13) | copy-start | bytes 1474564
  91.8 9.3 %collective-permute-start.4 = (bf16[4,96,1792]{2,1,0:T(8,128)(2,1)}, bf16[4,96,1792]{2,1,0:T(8,128)(2,1)}, u32[]{:S(2)}, u32[]{:S(2)}) collective-permute-start(bf16[4,96,1792]{2,1,0:T(8,128)(2,1)} %bitcast.12), channel_id=1, source_target_pairs={{0,1},{1,0},{2,3},{3,2},{4,5},{5,4},{6,7},{7,6},{8,9},{9,8},{10,11... | collective-permute-start | bytes 4128776 | tf_op jit(solution)/shard_map/ppermute | solution.py:22
  101.1 9.8 %copy-start = (bf16[16,12,640]{2,1,0:T(8,128)(2,1)S(1)}, bf16[16,12,640]{2,1,0:T(8,128)(2,1)}, u32[]{:S(2)}) copy-start(bf16[16,12,640]{2,1,0:T(8,128)(2,1)} %slice.59) | copy-start | bytes 737284
  102.8 14.0 %collective-permute-start.5 = (bf16[48,1792]{1,0:T(8,128)(2,1)S(1)}, bf16[48,1792]{1,0:T(8,128)(2,1)S(1)}, u32[]{:S(2)}, u32[]{:S(2)}) collective-permute-start(bf16[48,1792]{1,0:T(8,128)(2,1)S(1)} %get-tuple-element.8), channel_id=1, source_target_pairs={{0,2},{2,4},{4,6},{6,0},{1,3},{3,5},{5,7},{7,1},{8,10},{10,12},{12... | collective-permute-start | bytes 516104 | tf_op jit(solution)/shard_map/ppermute | solution.py:22
  106.9 11.7 %collective-permute-start.7 = (bf16[48,1792]{1,0:T(8,128)(2,1)S(1)}, bf16[48,1792]{1,0:T(8,128)(2,1)S(1)}, u32[]{:S(2)}, u32[]{:S(2)}) collective-permute-start(bf16[48,1792]{1,0:T(8,128)(2,1)S(1)} %get-tuple-element.9), channel_id=1, source_target_pairs={{0,6},{2,0},{4,2},{6,4},{1,7},{3,1},{5,3},{7,5},{8,14},{10,8},{12,... | collective-permute-start | bytes 516104 | tf_op jit(solution)/shard_map/ppermute | solution.py:22
  111.9 14.6 %copy-start.8 = (f32[192]{0:T(256)S(1)}, f32[192]{0:T(256)}, u32[]{:S(2)}) copy-start(f32[192]{0:T(256)} %param.9) | copy-start | bytes 2308
  111.9 17.3 %all-to-all-start.2 = ((bf16[4,16,12,640]{3,1,2,0:T(8,128)(2,1)}), bf16[4,16,12,640]{3,1,2,0:T(8,128)(2,1)S(1)}, u32[]{:S(2)}, u32[]{:S(2)}) async-start(bf16[4,16,12,640]{3,1,2,0:T(8,128)(2,1)} %broadcast_in_dim.48), calls=%async_computation.2 | async-start | bytes 1966080 | tf_op jit(solution)/shard_map/all_to_all | solution.py:27
  118.8 12.2 %collective-permute-start.8 = (bf16[96,1792]{1,0:T(8,128)(2,1)S(1)}, bf16[96,1792]{1,0:T(8,128)(2,1)S(1)}, u32[]{:S(2)}, u32[]{:S(2)}) collective-permute-start(bf16[96,1792]{1,0:T(8,128)(2,1)S(1)} %pad_maximum_fusion.2), channel_id=1, source_target_pairs={{0,6},{2,0},{4,2},{6,4},{1,7},{3,1},{5,3},{7,5},{8,14},{10,8},{12,... | collective-permute-start | bytes 1032200 | tf_op jit(solution)/shard_map/ppermute | solution.py:22
  124.6 18.8 %collective-permute-start.6 = (bf16[96,1792]{1,0:T(8,128)(2,1)}, bf16[96,1792]{1,0:T(8,128)(2,1)}, u32[]{:S(2)}, u32[]{:S(2)}) collective-permute-start(bf16[96,1792]{1,0:T(8,128)(2,1)} %pad_maximum_fusion.1), channel_id=1, source_target_pairs={{0,2},{2,4},{4,6},{6,0},{1,3},{3,5},{5,7},{7,1},{8,10},{10,12},{12... | collective-permute-start | bytes 1032200 | tf_op jit(solution)/shard_map/ppermute | solution.py:22
  130.5 23.1 %copy-start.3 = (bf16[8,96,432]{2,1,0:T(8,128)(2,1)S(1)}, bf16[8,96,432]{2,1,0:T(8,128)(2,1)}, u32[]{:S(2)}) copy-start(bf16[8,96,432]{2,1,0:T(8,128)(2,1)} %copy-done.2) | copy-start | bytes 1990660
  144.9 10.2 %collective-permute-start.9 = (bf16[96,436]{1,0:T(8,128)(2,1)S(1)}, bf16[96,436]{1,0:T(8,128)(2,1)S(1)}, u32[]{:S(2)}, u32[]{:S(2)}) collective-permute-start(bf16[96,436]{1,0:T(8,128)(2,1)S(1)} %get-tuple-element.20), channel_id=1, source_target_pairs={{0,16},{16,32},{32,48},{48,0},{1,17},{17,33},{33,49},{49,1},{2,18}... | collective-permute-start | bytes 251144 | tf_op jit(solution)/shard_map/ppermute | solution.py:22
  147.3 8.0 %collective-permute-start.10 = (bf16[96,436]{1,0:T(8,128)(2,1)S(1)}, bf16[96,436]{1,0:T(8,128)(2,1)S(1)}, u32[]{:S(2)}, u32[]{:S(2)}) collective-permute-start(bf16[96,436]{1,0:T(8,128)(2,1)S(1)} %get-tuple-element.21), channel_id=1, source_target_pairs={{0,32},{16,48},{32,0},{48,16},{1,33},{17,49},{33,1},{49,17},{2,34}... | collective-permute-start | bytes 251144 | tf_op jit(solution)/shard_map/ppermute | solution.py:22
  151.7 7.7 %collective-permute-start.11 = (bf16[96,436]{1,0:T(8,128)(2,1)S(1)}, bf16[96,436]{1,0:T(8,128)(2,1)S(1)}, u32[]{:S(2)}, u32[]{:S(2)}) collective-permute-start(bf16[96,436]{1,0:T(8,128)(2,1)S(1)} %concatenate.32), channel_id=1, source_target_pairs={{0,48},{16,0},{32,16},{48,32},{1,49},{17,1},{33,17},{49,33},{2,50}... | collective-permute-start | bytes 251144 | tf_op jit(solution)/shard_map/ppermute | solution.py:22
  153.6 6.9 %copy-start.5 = (bf16[96,432]{1,0:T(8,128)(2,1)S(1)}, bf16[96,432]{1,0:T(8,128)(2,1)}, u32[]{:S(2)}) copy-start(bf16[96,432]{1,0:T(8,128)(2,1)} %param.8) | copy-start | bytes 248836

commit v2 on v1

--- a/solution.py
+++ b/solution.py
@@ -1,8 +1,10 @@
-import itertools
+import functools
 
 import jax
 import jax.numpy as jnp
 from jax import lax
+from jax.experimental import pallas as pl
+from jax.experimental.pallas import tpu as pltpu
 from jax.sharding import Mesh
 from jax.sharding import PartitionSpec as P
 
@@ -37,12 +39,78 @@
     return lax.dot_general(a, b, (((1,), (1,)), ((), ())), preferred_element_type=jnp.float32)
 
 
+CHUNK = 256
+
+
+def partial_kernel(rows, factors, where_ref, *refs):
+    *near_refs, weight_ref, out_ref, token_ref = refs
+    step = pl.program_id(0)
+    slot = near_refs[0].shape[1] // 2
+    block = 2 * rows
+
+    @pl.when(step == 0)
+    def _():
+        for j, near in enumerate(near_refs):
+            token_ref[j * block : j * block + rows] = near[0, :rows]
+            token_ref[j * block + rows : (j + 1) * block] = near[0, slot : slot + rows]
+
+    product = dot_t(token_ref[...], weight_ref[...])
+
+    @pl.when(step < pl.num_programs(0) - 1)
+    def _():
+        out_ref[...] = product.reshape(out_ref.shape).astype(out_ref.dtype)
+
+    @pl.when(step == pl.num_programs(0) - 1)
+    def _():
+        row = lax.broadcasted_iota(jnp.int32, (block, 2 * slot), 0)
+        col = lax.broadcasted_iota(jnp.int32, (block, 2 * slot), 1)
+        place = col % slot - rows
+        same = (row // rows == col // slot) & (place >= 0) & (place < factors)
+        same &= row % rows // MEMBER_TOKENS == place // RANK
+        k = lax.broadcasted_iota(jnp.int32, (2 * slot, 128), 0)
+        c = lax.broadcasted_iota(jnp.int32, (2 * slot, 128), 1)
+        pick = jnp.where(c == 64 + k % RANK, 1.0, 0.0).astype(jnp.bfloat16)
+        for j, near in enumerate(near_refs):
+            projection = dot_t(token_ref[j * block : (j + 1) * block], near[0])
+            projection = jnp.where(same, projection, 0.0).astype(jnp.bfloat16)
+            tail = jnp.dot(projection, pick, preferred_element_type=jnp.float32)
+            part = product[j * block : (j + 1) * block]
+            out_ref[j, :, :128] = part[:, :128].astype(out_ref.dtype)
+            out_ref[j, :, 128:] = (part[:, 128:] + tail).astype(out_ref.dtype)
+
+
+def partials(near, weights, where, rows, factors):
+    n_hi = 4
+    wide, features = weights.shape
+    blocks = near.reshape(2 * n_hi, -1, features)
+
+    def near_spec(j):
+        return pl.BlockSpec((1, blocks.shape[1], features), lambda n, at: (2 * ((at[0] + j) % n_hi) + at[1], 0, 0))
+
+    return pl.pallas_call(
+        functools.partial(partial_kernel, rows, factors),
+        grid_spec=pltpu.PrefetchScalarGridSpec(
+            num_scalar_prefetch=1,
+            grid=(wide // CHUNK,),
+            in_specs=[near_spec(j) for j in range(n_hi)] + [pl.BlockSpec((CHUNK, features), lambda n, at: (n, 0))],
+            out_specs=pl.BlockSpec((n_hi, 2 * rows, CHUNK), lambda n, at: (0, 0, n)),
+            scratch_shapes=[pltpu.VMEM((n_hi * 2 * rows, features), jnp.bfloat16)],
+        ),
+        out_shape=jax.ShapeDtypeStruct((n_hi, 2 * rows, wide), jnp.bfloat16),
+        cost_estimate=pl.CostEstimate(
+            flops=2 * n_hi * 2 * rows * wide * features, transcendentals=0, bytes_accessed=2 * (wide * features + 2 * n_hi * rows * wide)
+        ),
+        compiler_params=pltpu.CompilerParams(dimension_semantics=("arbitrary",)),
+    )(where, *[blocks] * n_hi, weights)
+
+
 def body(tokens, up_weight, left_factors, right_factors, fitness):
     f32, bf16 = jnp.float32, jnp.bfloat16
     hi, core, x = lax.axis_index("hi"), lax.axis_index("core"), lax.axis_index("x")
     rows, features = tokens.shape
     factors = left_factors.shape[0]
     columns = up_weight.shape[1]
+    own = right_factors.shape[0]
     n_x, n_hi, n_z, n_lo = (lax.axis_size(a) for a in ("x", "hi", "z", "lo"))
     wide = -(-(n_x * columns + RANK) // 128) * 128
 
@@ -59,34 +127,22 @@
         ],
         0,
     )
-    right_all = gathered(right_factors, TENSOR)
-    near, right_all = lax.optimization_barrier((near, right_all))
+    right_after = shifted(right_factors, "hi", -1)
+    right_before = shifted(right_factors, "hi", 1)
+    low = own // 2
+    right_far = jnp.concatenate([shifted(right_before[:low], "hi", 1), shifted(right_after[low:], "hi", -1)], 0)
+    right_same = jnp.stack([right_factors, right_after, right_far, right_before])
+    near, right_same = lax.optimization_barrier((near, right_same))
     near_left = near[:, rows : rows + factors]
     weights = jnp.concatenate(
         [weight, weight_after, weight_far, weight_before, jnp.zeros((wide - n_x * columns, features), bf16)], 0
     )
 
     block = n_lo * rows
-    token_blocks = near[:, :rows].reshape(n_hi, 2, block, features)
-    left_blocks = near_left.reshape(n_hi, 2, n_lo * factors, features)
-    row = lax.broadcasted_iota(jnp.int32, (n_hi * block, n_hi * n_lo * factors), 0)
-    col = lax.broadcasted_iota(jnp.int32, (n_hi * block, n_hi * n_lo * factors), 1)
-    same = row // MEMBER_TOKENS == col // RANK
-    k = lax.broadcasted_iota(jnp.int32, (wide, n_hi * n_lo * factors), 1)
-    c = lax.broadcasted_iota(jnp.int32, (wide, n_hi * n_lo * factors), 0)
-    place = (c == n_x * columns + k % RANK).astype(bf16)
-
-    def partial(side):
-        some = wrapped(lax.dynamic_index_in_dim(token_blocks, side, 1, False), hi)
-        lefts = wrapped(lax.dynamic_index_in_dim(left_blocks, side, 1, False), hi)
-        some = some.reshape(n_hi * block, features)
-        lefts = lefts.reshape(-1, features)
-        projection = jnp.where(same, dot_t(some, lefts), 0.0).astype(bf16)
-        return (dot_t(some, weights) + dot_t(projection, place)).reshape(n_hi, block, wide)
-
-    sent = partial(1 - core).astype(bf16)
+    sent = partials(near, weights, jnp.stack([hi, 1 - core]), rows, factors)
     other = shifted(sent, "core", 1)
-    both = (partial(core) + other.astype(f32)).astype(bf16)
+    kept = partials(near, weights, jnp.stack([hi, core]), rows, factors)
+    both = (kept.astype(f32) + other.astype(f32)).astype(bf16)
     cut = block // 2
     via_after = shifted(both[2, :cut], "hi", 1)
     via_before = shifted(both[2, cut:], "hi", -1)
@@ -101,14 +157,11 @@
     total = both[0].astype(f32) + from_before.astype(f32) + from_after.astype(f32)
     total = total.astype(bf16)
 
-    pieces = []
-    for j in range(n_x):
-        piece = jnp.concatenate(
-            [total[:, j * columns : (j + 1) * columns], total[:, n_x * columns : n_x * columns + RANK]], 1
-        )
-        pieces.append(shifted(piece, "x", j) if j else piece)
-    whole = wrapped(jnp.stack(pieces), x, -1).reshape(n_x * block, columns + RANK)
-    own = right_factors.shape[0]
+    tail = total[:, n_x * columns : n_x * columns + RANK]
+    pieces = [jnp.concatenate([total[:, j * columns : (j + 1) * columns], tail], 1) for j in range(n_x)]
+    pieces = wrapped(jnp.stack(pieces), n_x - x)
+    whole = lax.all_to_all(pieces, "x", split_axis=0, concat_axis=0, tiled=True)
+    whole = whole.reshape(n_x * block, columns + RANK)
     row = lax.broadcasted_iota(jnp.int32, (n_x * block, own), 0)
     col = lax.broadcasted_iota(jnp.int32, (n_x * block, own), 1)
     tiled = jnp.tile(whole[:, columns:], (1, own // RANK))
@@ -121,7 +174,10 @@
     left_all = left_all.reshape(-1, features)
     fit = jnp.repeat(fitness, RANK)
     weighted = (fit[:, None] * left_all.astype(f32)).astype(bf16)
-    right_all = right_all.reshape(-1, columns)
+    right_other = shifted(right_same, "core", 1)
+    here = core == 0
+    right_all = jnp.stack([jnp.where(here, right_same, right_other), jnp.where(here, right_other, right_same)], 1)
+    right_all = wrapped(right_all, n_hi - hi).reshape(-1, columns)
     gradient = jnp.einsum("kd,kf->df", weighted, right_all, preferred_element_type=f32)
     return hidden, (gradient * GRADIENT_SCALE).astype(bf16)
 

time: 163 us -> 154 us (0.945)
  the two profiles are of different devices: /device:TPU:6 before, /device:TPU:136 now
where the time goes in v2:
time: 154 us; the launch traced here: 152 us
  starting transfers between devices  68.3 us (44%)
  waiting for transfers between devices  38.3 us (25%)
  Pallas kernels  16.6 us (11%)
  local copies, waits for them, and re-layouts  14.9 us (10%)
  other arithmetic  10.7 us (7%)
  matrix products  2.61 us (2%)
    ppermute x14, starting transfers between devices, shifted(): lax.ppermute(array, axis, [(k, (k + step) % size) for k in range(size)])  49.4 us
    ppermute x14, waiting for transfers between devices, shifted(): lax.ppermute(array, axis, [(k, (k + step) % size) for k in range(size)])  32.5 us
    pallas_call x2, Pallas kernels, partials(): pl.pallas_call(functools.partial(partial_kernel, rows, factors), grid_spe...  16.6 us
    all_to_all x2, starting transfers between devices, gathered(): return lax.all_to_all(copies, axes, split_axis=0, concat_axis=0, tiled=True)  14.2 us
    all_to_all x1, waiting for transfers between devices, body(): whole = lax.all_to_all(pieces, 'x', split_axis=0, concat_axis=0, tiled=True)  5.84 us
    unnamed x30, local copies, waits for them, and re-layouts  5.43 us
    all_to_all x1, starting transfers between devices, body(): whole = lax.all_to_all(pieces, 'x', split_axis=0, concat_axis=0, tiled=True)  4.66 us
  transfers between devices with their start and end apart: 17, of which 8 were waited for; matrix products, arithmetic and copies ran while one was open for 13% of the time, Pallas kernels for 5%

profile of v2, /device:TPU:136, one launch (start us, length us, event | category | flops | bytes accessed | tf_op | source)
XLA Modules:
  0.0 152.5 jit_solution(16292913944842994847)
XLA Ops:
  0.7 1.0 maximum_maximum_fusion
  1.7 1.2 broadcast_in_dim.28
  2.9 10.0 %all-to-all-start = ((bf16[16,64,640]{2,1,0:T(8,128)(2,1)}), bf16[16,64,640]{2,1,0:T(8,128)(2,1)S(1)}, u32[]{:S(2)}, u32[]{:S(2)}) async-start(bf16[16,64,640]{2,1,0:T(8,128)(2,1)} %broadcast_in_dim.28), calls=%async_computation | async-start | bytes 2621440 | tf_op jit(solution)/shard_map/all_to_all | solution.py:29
  12.9 3.4 %collective-permute-start.5 = (bf16[432,640]{1,0:T(8,128)(2,1)S(1)}, bf16[432,640]{1,0:T(8,128)(2,1)S(1)}, u32[]{:S(2)}, u32[]{:S(2)}) collective-permute-start(bf16[432,640]{1,0:T(8,128)(2,1)S(1)} %bitcast.76), channel_id=1, source_target_pairs={{0,16},{16,32},{32,48},{48,0},{1,17},{17,33},{33,49},{49,1},{2,18}... | collective-permute-start | bytes 1658888 | tf_op jit(solution)/shard_map/ppermute | solution.py:24
  16.3 3.7 %collective-permute-start.4 = (bf16[432,640]{1,0:T(8,128)(2,1)S(1)}, bf16[432,640]{1,0:T(8,128)(2,1)S(1)}, u32[]{:S(2)}, u32[]{:S(2)}) collective-permute-start(bf16[432,640]{1,0:T(8,128)(2,1)S(1)} %bitcast.77), channel_id=1, source_target_pairs={{0,48},{16,0},{32,16},{48,32},{1,49},{17,1},{33,17},{49,33},{2,50}... | collective-permute-start | bytes 1658888 | tf_op jit(solution)/shard_map/ppermute | solution.py:24
  20.0 4.5 %collective-permute-start.1 = (bf16[96,432]{1,0:T(8,128)(2,1)S(1)}, bf16[96,432]{1,0:T(8,128)(2,1)S(1)}, u32[]{:S(2)}, u32[]{:S(2)}) collective-permute-start(bf16[96,432]{1,0:T(8,128)(2,1)S(1)} %copy-done.5), channel_id=1, source_target_pairs={{0,2},{2,4},{4,6},{6,0},{1,3},{3,5},{5,7},{7,1},{8,10},{10,12},{12... | collective-permute-start | bytes 248840 | tf_op jit(solution)/shard_map/ppermute | solution.py:24
  24.5 3.5 %collective-permute-start = (bf16[96,432]{1,0:T(8,128)(2,1)S(1)}, bf16[96,432]{1,0:T(8,128)(2,1)S(1)}, u32[]{:S(2)}, u32[]{:S(2)}) collective-permute-start(bf16[96,432]{1,0:T(8,128)(2,1)S(1)} %copy-done.5), channel_id=1, source_target_pairs={{0,6},{2,0},{4,2},{6,4},{1,7},{3,1},{5,3},{7,5},{8,14},{10,8},{12,... | collective-permute-start | bytes 248840 | tf_op jit(solution)/shard_map/ppermute | solution.py:24
  28.0 0.8 constant_dynamic-update-slice_fusion.4
  28.8 3.3 %collective-permute-start.2 = (bf16[48,432]{1,0:T(8,128)(2,1)S(1)}, bf16[48,432]{1,0:T(8,128)(2,1)S(1)}, u32[]{:S(2)}, u32[]{:S(2)}) collective-permute-start(bf16[48,432]{1,0:T(8,128)(2,1)S(1)} %slice.78), channel_id=1, source_target_pairs={{0,2},{2,4},{4,6},{6,0},{1,3},{3,5},{5,7},{7,1},{8,10},{10,12},{12... | collective-permute-start | bytes 124424 | tf_op jit(solution)/shard_map/ppermute | solution.py:24
  32.1 9.3 %collective-permute-done = bf16[96,432]{1,0:T(8,128)(2,1)S(1)} collective-permute-done((bf16[96,432]{1,0:T(8,128)(2,1)S(1)}, bf16[96,432]{1,0:T(8,128)(2,1)S(1)}, u32[]{:S(2)}, u32[]{:S(2)}) %collective-permute-start) | collective-permute-done | bytes 82976 | tf_op jit(solution)/shard_map/ppermute | solution.py:24
  41.4 3.3 %collective-permute-start.3 = (bf16[48,432]{1,0:T(8,128)(2,1)S(1)}, bf16[48,432]{1,0:T(8,128)(2,1)S(1)}, u32[]{:S(2)}, u32[]{:S(2)}) collective-permute-start(bf16[48,432]{1,0:T(8,128)(2,1)S(1)} %slice.79), channel_id=1, source_target_pairs={{0,6},{2,0},{4,2},{6,4},{1,7},{3,1},{5,3},{7,5},{8,14},{10,8},{12,... | collective-permute-start | bytes 124424 | tf_op jit(solution)/shard_map/ppermute | solution.py:24
  45.4 3.5 %collective-permute-start.6 = (bf16[216,640]{1,0:T(8,128)(2,1)S(1)}, bf16[216,640]{1,0:T(8,128)(2,1)S(1)}, u32[]{:S(2)}, u32[]{:S(2)}) collective-permute-start(bf16[216,640]{1,0:T(8,128)(2,1)S(1)} %slice.80), channel_id=1, source_target_pairs={{0,16},{16,32},{32,48},{48,0},{1,17},{17,33},{33,49},{49,1},{2,18}... | collective-permute-start | bytes 829448 | tf_op jit(solution)/shard_map/ppermute | solution.py:24
  49.0 3.9 %collective-permute-start.7 = (bf16[216,640]{1,0:T(8,128)(2,1)S(1)}, bf16[216,640]{1,0:T(8,128)(2,1)S(1)}, u32[]{:S(2)}, u32[]{:S(2)}) collective-permute-start(bf16[216,640]{1,0:T(8,128)(2,1)S(1)} %slice.81), channel_id=1, source_target_pairs={{0,48},{16,0},{32,16},{48,32},{1,49},{17,1},{33,17},{49,33},{2,50}... | collective-permute-start | bytes 829448 | tf_op jit(solution)/shard_map/ppermute | solution.py:24
  52.9 1.0 pad_maximum_fusion.1
  53.9 0.9 constant_dynamic-update-slice_fusion.3
  54.8 0.8 collective-permute-done.6
  55.6 0.7 constant_dynamic-update-slice_fusion.2
  56.3 1.4 collective-permute-done.7
  57.7 0.8 constant_dynamic-update-slice_fusion.1
  58.5 0.9 constant_dynamic-update-slice_fusion
  59.9 1.1 copy-done
  61.0 8.4 %shard_map.69 = bf16[4,96,1792]{2,1,0:T(8,128)(2,1)} custom-call(s32[2]{0:T(128)} %pad_add_fusion.1.where_ref, bf16[8,128,640]{2,1,0:T(8,128)(2,1)} %bitcast.63, bf16[8,128,640]{2,1,0:T(8,128)(2,1)} %bitcast.64, bf16[8,128,640]{2,1,0:T(8,128)(2,1)} %bitcast.65, bf16[8,128,640]{2,1,0:T(8,128)(2,1)} %bitcast.66, ...), custom_call_target="tpu_custom_call" | custom-call | flops 880803840 | bytes 3670016 | tf_op jit(solution)/shard_map/pallas_call | solution.py:90
  69.4 1.9 %collective-permute-start.8 = (bf16[4,96,1792]{2,1,0:T(8,128)(2,1)}, bf16[4,96,1792]{2,1,0:T(8,128)(2,1)}, u32[]{:S(2)}, u32[]{:S(2)}) collective-permute-start(bf16[4,96,1792]{2,1,0:T(8,128)(2,1)} %shard_map.69), channel_id=1, source_target_pairs={{0,1},{1,0},{2,3},{3,2},{4,5},{5,4},{6,7},{7,6},{8,9},{9,8},{10,11... | collective-permute-start | bytes 4128776 | tf_op jit(solution)/shard_map/ppermute | solution.py:24
  71.6 0.9 copy.26
  74.8 1.0 slice.73
  75.9 2.4 %collective-permute-start.13 = (bf16[4,96,432]{2,1,0:T(8,128)(2,1)S(1)}, bf16[4,96,432]{2,1,0:T(8,128)(2,1)S(1)}, u32[]{:S(2)}, u32[]{:S(2)}) collective-permute-start(bf16[4,96,432]{2,1,0:T(8,128)(2,1)S(1)} %pad_maximum_fusion.1), channel_id=1, source_target_pairs={{0,1},{1,0},{2,3},{3,2},{4,5},{5,4},{6,7},{7,6},{8,9},{9,8},{10,11... | collective-permute-start | bytes 995336 | tf_op jit(solution)/shard_map/ppermute | solution.py:24
  78.3 1.1 broadcast_in_dim.34
  79.4 4.2 %all-to-all-start.2 = ((bf16[4,16,12,640]{3,1,2,0:T(8,128)(2,1)}), bf16[4,16,12,640]{3,1,2,0:T(8,128)(2,1)S(1)}, u32[]{:S(2)}, u32[]{:S(2)}) async-start(bf16[4,16,12,640]{3,1,2,0:T(8,128)(2,1)} %broadcast_in_dim.34), calls=%async_computation.2 | async-start | bytes 1966080 | tf_op jit(solution)/shard_map/all_to_all | solution.py:29
  83.6 8.3 %shard_map.68 = bf16[4,96,1792]{2,1,0:T(8,128)(2,1)} custom-call(s32[2]{0:T(128)} %pad_add_fusion.where_ref, bf16[8,128,640]{2,1,0:T(8,128)(2,1)} %bitcast.67, bf16[8,128,640]{2,1,0:T(8,128)(2,1)} %bitcast.68, bf16[8,128,640]{2,1,0:T(8,128)(2,1)} %bitcast.69, bf16[8,128,640]{2,1,0:T(8,128)(2,1)} %bitcast.70, ...), custom_call_target="tpu_custom_call" | custom-call | flops 880803840 | bytes 3670016 | tf_op jit(solution)/shard_map/pallas_call | solution.py:90
  91.9 2.1 %add_convert_fusion = bf16[4,96,1792]{2,1,0:T(8,128)(2,1)S(1)} fusion(bf16[4,96,1792]{2,1,0:T(8,128)(2,1)} %collective-permute-done.8, bf16[4,96,1792]{2,1,0:T(8,128)(2,1)} %shard_map.68), kind=kLoop, calls=%fused_computation.2 | loop fusion | flops 2752512 | bytes 4128768 | tf_op jit(solution)/shard_map/convert_element_type | solution.py:145
  94.0 4.9 %collective-permute-start.11 = (bf16[48,1792]{1,0:T(8,128)(2,1)S(1)}, bf16[48,1792]{1,0:T(8,128)(2,1)S(1)}, u32[]{:S(2)}, u32[]{:S(2)}) collective-permute-start(bf16[48,1792]{1,0:T(8,128)(2,1)S(1)} %get-tuple-element.9), channel_id=1, source_target_pairs={{0,6},{2,0},{4,2},{6,4},{1,7},{3,1},{5,3},{7,5},{8,14},{10,8},{12,... | collective-permute-start | bytes 516104 | tf_op jit(solution)/shard_map/ppermute | solution.py:24
  98.9 3.1 %collective-permute-start.9 = (bf16[48,1792]{1,0:T(8,128)(2,1)S(1)}, bf16[48,1792]{1,0:T(8,128)(2,1)S(1)}, u32[]{:S(2)}, u32[]{:S(2)}) collective-permute-start(bf16[48,1792]{1,0:T(8,128)(2,1)S(1)} %get-tuple-element.8), channel_id=1, source_target_pairs={{0,2},{2,4},{4,6},{6,0},{1,3},{3,5},{5,7},{7,1},{8,10},{10,12},{12... | collective-permute-start | bytes 516104 | tf_op jit(solution)/shard_map/ppermute | solution.py:24
  102.1 2.3 %collective-permute-done.11 = bf16[48,1792]{1,0:T(8,128)(2,1)S(1)} collective-permute-done((bf16[48,1792]{1,0:T(8,128)(2,1)S(1)}, bf16[48,1792]{1,0:T(8,128)(2,1)S(1)}, u32[]{:S(2)}, u32[]{:S(2)}) %collective-permute-start.11) | collective-permute-done | bytes 172064 | tf_op jit(solution)/shard_map/ppermute | solution.py:24
  104.4 4.3 %collective-permute-done.9 = bf16[48,1792]{1,0:T(8,128)(2,1)S(1)} collective-permute-done((bf16[48,1792]{1,0:T(8,128)(2,1)S(1)}, bf16[48,1792]{1,0:T(8,128)(2,1)S(1)}, u32[]{:S(2)}, u32[]{:S(2)}) %collective-permute-start.9) | collective-permute-done | bytes 172064 | tf_op jit(solution)/shard_map/ppermute | solution.py:24
  108.8 0.8 pad_maximum_fusion.3
  109.6 6.2 %collective-permute-start.10 = (bf16[96,1792]{1,0:T(8,128)(2,1)}, bf16[96,1792]{1,0:T(8,128)(2,1)}, u32[]{:S(2)}, u32[]{:S(2)}) collective-permute-start(bf16[96,1792]{1,0:T(8,128)(2,1)} %pad_maximum_fusion.3), channel_id=1, source_target_pairs={{0,2},{2,4},{4,6},{6,0},{1,3},{3,5},{5,7},{7,1},{8,10},{10,12},{12... | collective-permute-start | bytes 1032200 | tf_op jit(solution)/shard_map/ppermute | solution.py:24
  115.8 0.8 pad_maximum_fusion.4
  116.6 1.9 %collective-permute-start.12 = (bf16[96,1792]{1,0:T(8,128)(2,1)}, bf16[96,1792]{1,0:T(8,128)(2,1)}, u32[]{:S(2)}, u32[]{:S(2)}) collective-permute-start(bf16[96,1792]{1,0:T(8,128)(2,1)} %pad_maximum_fusion.4), channel_id=1, source_target_pairs={{0,6},{2,0},{4,2},{6,4},{1,7},{3,1},{5,3},{7,5},{8,14},{10,8},{12,... | collective-permute-start | bytes 1032200 | tf_op jit(solution)/shard_map/ppermute | solution.py:24
  118.6 1.5 gather_fusion.1
  120.1 0.8 copy.28
  121.5 2.6 %collective-permute-done.10 = bf16[96,1792]{1,0:T(8,128)(2,1)} collective-permute-done((bf16[96,1792]{1,0:T(8,128)(2,1)}, bf16[96,1792]{1,0:T(8,128)(2,1)}, u32[]{:S(2)}, u32[]{:S(2)}) %collective-permute-start.10) | collective-permute-done | bytes 344096 | tf_op jit(solution)/shard_map/ppermute | solution.py:24
  124.0 11.8 %collective-permute-done.12 = bf16[96,1792]{1,0:T(8,128)(2,1)} collective-permute-done((bf16[96,1792]{1,0:T(8,128)(2,1)}, bf16[96,1792]{1,0:T(8,128)(2,1)}, u32[]{:S(2)}, u32[]{:S(2)}) %collective-permute-start.12) | collective-permute-done | bytes 344096 | tf_op jit(solution)/shard_map/ppermute | solution.py:24
  135.9 1.2 fusion.4
  137.5 1.3 gather_fusion
  138.8 4.7 %all-to-all-start.1 = ((bf16[4,96,436]{2,1,0:T(8,128)(2,1)}), bf16[4,96,436]{2,1,0:T(8,128)(2,1)S(1)}, u32[]{:S(2)}, u32[]{:S(2)}) async-start(bf16[4,96,436]{2,1,0:T(8,128)(2,1)} %gather_fusion), calls=%async_computation.1 | async-start | bytes 786432 | tf_op jit(solution)/shard_map/all_to_all | solution.py:163
  143.5 1.5 %fusion = bf16[640,432]{0,1:T(8,128)(2,1)} fusion(bf16[768,640]{1,0:T(8,128)(2,1)S(1)} %bitcast.74, bf16[768,432]{1,0:T(8,128)(2,1)S(1)} %bitcast.75), kind=kOutput, calls=%fused_computation.5 | convolution fusion | flops 425226240 | bytes 2199552 | tf_op jit(solution)/shard_map/kd,kf->df/dot_general | solution.py:181
  145.0 5.8 %all-to-all-done.1 = bf16[4,96,436]{2,1,0:T(8,128)(2,1)S(1)} async-done(((bf16[4,96,436]{2,1,0:T(8,128)(2,1)}), bf16[4,96,436]{2,1,0:T(8,128)(2,1)S(1)}, u32[]{:S(2)}, u32[]{:S(2)}) %all-to-all-start.1) | async-done | bytes 334880 | tf_op jit(solution)/shard_map/all_to_all | solution.py:163
  151.4 1.1 fusion.2
  (68 shorter events, 5.9 us)
Async XLA Ops:
  0.6 12.3 %copy-start.2 = (bf16[640,432]{0,1:T(8,128)(2,1)S(1)}, bf16[640,432]{0,1:T(8,128)(2,1)}, u32[]{:S(2)}) copy-start(bf16[640,432]{0,1:T(8,128)(2,1)} %param.6) | copy-start | bytes 1658884
  0.6 19.4 %copy-start.5 = (bf16[96,432]{1,0:T(8,128)(2,1)S(1)}, bf16[96,432]{1,0:T(8,128)(2,1)}, u32[]{:S(2)}) copy-start(bf16[96,432]{1,0:T(8,128)(2,1)} %param.8) | copy-start | bytes 248836
  2.9 57.0 %all-to-all-start = ((bf16[16,64,640]{2,1,0:T(8,128)(2,1)}), bf16[16,64,640]{2,1,0:T(8,128)(2,1)S(1)}, u32[]{:S(2)}, u32[]{:S(2)}) async-start(bf16[16,64,640]{2,1,0:T(8,128)(2,1)} %broadcast_in_dim.28), calls=%async_computation | async-start | bytes 2621440 | tf_op jit(solution)/shard_map/all_to_all | solution.py:29
  12.9 32.4 %collective-permute-start.5 = (bf16[432,640]{1,0:T(8,128)(2,1)S(1)}, bf16[432,640]{1,0:T(8,128)(2,1)S(1)}, u32[]{:S(2)}, u32[]{:S(2)}) collective-permute-start(bf16[432,640]{1,0:T(8,128)(2,1)S(1)} %bitcast.76), channel_id=1, source_target_pairs={{0,16},{16,32},{32,48},{48,0},{1,17},{17,33},{33,49},{49,1},{2,18}... | collective-permute-start | bytes 1658888 | tf_op jit(solution)/shard_map/ppermute | solution.py:24
  16.3 32.6 %collective-permute-start.4 = (bf16[432,640]{1,0:T(8,128)(2,1)S(1)}, bf16[432,640]{1,0:T(8,128)(2,1)S(1)}, u32[]{:S(2)}, u32[]{:S(2)}) collective-permute-start(bf16[432,640]{1,0:T(8,128)(2,1)S(1)} %bitcast.77), channel_id=1, source_target_pairs={{0,48},{16,0},{32,16},{48,32},{1,49},{17,1},{33,17},{49,33},{2,50}... | collective-permute-start | bytes 1658888 | tf_op jit(solution)/shard_map/ppermute | solution.py:24
  20.0 8.8 %collective-permute-start.1 = (bf16[96,432]{1,0:T(8,128)(2,1)S(1)}, bf16[96,432]{1,0:T(8,128)(2,1)S(1)}, u32[]{:S(2)}, u32[]{:S(2)}) collective-permute-start(bf16[96,432]{1,0:T(8,128)(2,1)S(1)} %copy-done.5), channel_id=1, source_target_pairs={{0,2},{2,4},{4,6},{6,0},{1,3},{3,5},{5,7},{7,1},{8,10},{10,12},{12... | collective-permute-start | bytes 248840 | tf_op jit(solution)/shard_map/ppermute | solution.py:24
  24.5 16.9 %collective-permute-start = (bf16[96,432]{1,0:T(8,128)(2,1)S(1)}, bf16[96,432]{1,0:T(8,128)(2,1)S(1)}, u32[]{:S(2)}, u32[]{:S(2)}) collective-permute-start(bf16[96,432]{1,0:T(8,128)(2,1)S(1)} %copy-done.5), channel_id=1, source_target_pairs={{0,6},{2,0},{4,2},{6,4},{1,7},{3,1},{5,3},{7,5},{8,14},{10,8},{12,... | collective-permute-start | bytes 248840 | tf_op jit(solution)/shard_map/ppermute | solution.py:24
  28.8 20.1 %collective-permute-start.2 = (bf16[48,432]{1,0:T(8,128)(2,1)S(1)}, bf16[48,432]{1,0:T(8,128)(2,1)S(1)}, u32[]{:S(2)}, u32[]{:S(2)}) collective-permute-start(bf16[48,432]{1,0:T(8,128)(2,1)S(1)} %slice.78), channel_id=1, source_target_pairs={{0,2},{2,4},{4,6},{6,0},{1,3},{3,5},{5,7},{7,1},{8,10},{10,12},{12... | collective-permute-start | bytes 124424 | tf_op jit(solution)/shard_map/ppermute | solution.py:24
  41.4 11.5 %copy-start.4 = (bf16[96,432]{1,0:T(8,128)(2,1)}, bf16[96,432]{1,0:T(8,128)(2,1)S(1)}, u32[]{:S(2)}) copy-start(bf16[96,432]{1,0:T(8,128)(2,1)S(1)} %collective-permute-done) | copy-start | bytes 248836
  41.4 7.5 %collective-permute-start.3 = (bf16[48,432]{1,0:T(8,128)(2,1)S(1)}, bf16[48,432]{1,0:T(8,128)(2,1)S(1)}, u32[]{:S(2)}, u32[]{:S(2)}) collective-permute-start(bf16[48,432]{1,0:T(8,128)(2,1)S(1)} %slice.79), channel_id=1, source_target_pairs={{0,6},{2,0},{4,2},{6,4},{1,7},{3,1},{5,3},{7,5},{8,14},{10,8},{12,... | collective-permute-start | bytes 124424 | tf_op jit(solution)/shard_map/ppermute | solution.py:24
  45.4 10.2 %collective-permute-start.6 = (bf16[216,640]{1,0:T(8,128)(2,1)S(1)}, bf16[216,640]{1,0:T(8,128)(2,1)S(1)}, u32[]{:S(2)}, u32[]{:S(2)}) collective-permute-start(bf16[216,640]{1,0:T(8,128)(2,1)S(1)} %slice.80), channel_id=1, source_target_pairs={{0,16},{16,32},{32,48},{48,0},{1,17},{17,33},{33,49},{49,1},{2,18}... | collective-permute-start | bytes 829448 | tf_op jit(solution)/shard_map/ppermute | solution.py:24
  49.0 8.7 %collective-permute-start.7 = (bf16[216,640]{1,0:T(8,128)(2,1)S(1)}, bf16[216,640]{1,0:T(8,128)(2,1)S(1)}, u32[]{:S(2)}, u32[]{:S(2)}) collective-permute-start(bf16[216,640]{1,0:T(8,128)(2,1)S(1)} %slice.81), channel_id=1, source_target_pairs={{0,48},{16,0},{32,16},{48,32},{1,49},{17,1},{33,17},{49,33},{2,50}... | collective-permute-start | bytes 829448 | tf_op jit(solution)/shard_map/ppermute | solution.py:24
  59.9 1.1 copy-start
  61.0 10.3 %copy-start.7 = (f32[192]{0:T(256)S(1)}, f32[192]{0:T(256)}, u32[]{:S(2)}) copy-start(f32[192]{0:T(256)} %param.9) | copy-start | bytes 2308
  69.4 22.5 %collective-permute-start.8 = (bf16[4,96,1792]{2,1,0:T(8,128)(2,1)}, bf16[4,96,1792]{2,1,0:T(8,128)(2,1)}, u32[]{:S(2)}, u32[]{:S(2)}) collective-permute-start(bf16[4,96,1792]{2,1,0:T(8,128)(2,1)} %shard_map.69), channel_id=1, source_target_pairs={{0,1},{1,0},{2,3},{3,2},{4,5},{5,4},{6,7},{7,6},{8,9},{9,8},{10,11... | collective-permute-start | bytes 4128776 | tf_op jit(solution)/shard_map/ppermute | solution.py:24
  75.9 26.1 %collective-permute-start.13 = (bf16[4,96,432]{2,1,0:T(8,128)(2,1)S(1)}, bf16[4,96,432]{2,1,0:T(8,128)(2,1)S(1)}, u32[]{:S(2)}, u32[]{:S(2)}) collective-permute-start(bf16[4,96,432]{2,1,0:T(8,128)(2,1)S(1)} %pad_maximum_fusion.1), channel_id=1, source_target_pairs={{0,1},{1,0},{2,3},{3,2},{4,5},{5,4},{6,7},{7,6},{8,9},{9,8},{10,11... | collective-permute-start | bytes 995336 | tf_op jit(solution)/shard_map/ppermute | solution.py:24
  79.4 40.6 %all-to-all-start.2 = ((bf16[4,16,12,640]{3,1,2,0:T(8,128)(2,1)}), bf16[4,16,12,640]{3,1,2,0:T(8,128)(2,1)S(1)}, u32[]{:S(2)}, u32[]{:S(2)}) async-start(bf16[4,16,12,640]{3,1,2,0:T(8,128)(2,1)} %broadcast_in_dim.34), calls=%async_computation.2 | async-start | bytes 1966080 | tf_op jit(solution)/shard_map/all_to_all | solution.py:29
  94.0 10.4 %collective-permute-start.11 = (bf16[48,1792]{1,0:T(8,128)(2,1)S(1)}, bf16[48,1792]{1,0:T(8,128)(2,1)S(1)}, u32[]{:S(2)}, u32[]{:S(2)}) collective-permute-start(bf16[48,1792]{1,0:T(8,128)(2,1)S(1)} %get-tuple-element.9), channel_id=1, source_target_pairs={{0,6},{2,0},{4,2},{6,4},{1,7},{3,1},{5,3},{7,5},{8,14},{10,8},{12,... | collective-permute-start | bytes 516104 | tf_op jit(solution)/shard_map/ppermute | solution.py:24
  98.9 9.8 %collective-permute-start.9 = (bf16[48,1792]{1,0:T(8,128)(2,1)S(1)}, bf16[48,1792]{1,0:T(8,128)(2,1)S(1)}, u32[]{:S(2)}, u32[]{:S(2)}) collective-permute-start(bf16[48,1792]{1,0:T(8,128)(2,1)S(1)} %get-tuple-element.8), channel_id=1, source_target_pairs={{0,2},{2,4},{4,6},{6,0},{1,3},{3,5},{5,7},{7,1},{8,10},{10,12},{12... | collective-permute-start | bytes 516104 | tf_op jit(solution)/shard_map/ppermute | solution.py:24
  109.6 14.5 %collective-permute-start.10 = (bf16[96,1792]{1,0:T(8,128)(2,1)}, bf16[96,1792]{1,0:T(8,128)(2,1)}, u32[]{:S(2)}, u32[]{:S(2)}) collective-permute-start(bf16[96,1792]{1,0:T(8,128)(2,1)} %pad_maximum_fusion.3), channel_id=1, source_target_pairs={{0,2},{2,4},{4,6},{6,0},{1,3},{3,5},{5,7},{7,1},{8,10},{10,12},{12... | collective-permute-start | bytes 1032200 | tf_op jit(solution)/shard_map/ppermute | solution.py:24
  116.6 19.3 %collective-permute-start.12 = (bf16[96,1792]{1,0:T(8,128)(2,1)}, bf16[96,1792]{1,0:T(8,128)(2,1)}, u32[]{:S(2)}, u32[]{:S(2)}) collective-permute-start(bf16[96,1792]{1,0:T(8,128)(2,1)} %pad_maximum_fusion.4), channel_id=1, source_target_pairs={{0,6},{2,0},{4,2},{6,4},{1,7},{3,1},{5,3},{7,5},{8,14},{10,8},{12,... | collective-permute-start | bytes 1032200 | tf_op jit(solution)/shard_map/ppermute | solution.py:24
  118.6 2.3 %copy-start.3 = (f32[8,4,24]{1,2,0:T(8,128)S(1)}, f32[8,4,24]{1,2,0:T(8,128)}, u32[]{:S(2)}) copy-start(f32[8,4,24]{1,2,0:T(8,128)} %copy.26) | copy-start | bytes 9220
  121.4 22.1 %copy-start.1 = (bf16[4,2,96,432]{3,2,1,0:T(8,128)(2,1)S(1)}, bf16[4,2,96,432]{3,2,1,0:T(8,128)(2,1)}, u32[]{:S(2)}) copy-start(bf16[4,2,96,432]{3,2,1,0:T(8,128)(2,1)} %gather_fusion.1) | copy-start | bytes 1990660
  138.8 12.6 %copy-start.6 = (bf16[96,432]{1,0:T(8,128)(2,1)S(1)}, bf16[96,432]{1,0:T(8,128)(2,1)}, u32[]{:S(2)}) copy-start(bf16[96,432]{1,0:T(8,128)(2,1)} %param.8) | copy-start | bytes 248836
  138.8 12.6 %copy-start.8 = (s32[96]{0:T(128)S(1)}, s32[96]{0:T(128)}, u32[]{:S(2)}) copy-start(s32[96]{0:T(128)} %get-tuple-element.25) | copy-start | bytes 1156
  138.8 12.6 %copy-start.9 = (s32[96]{0:T(128)S(1)}, s32[96]{0:T(128)}, u32[]{:S(2)}) copy-start(s32[96]{0:T(128)} %get-tuple-element.26) | copy-start | bytes 1156
  138.8 12.6 %copy-start.10 = (pred[96]{0:T(512)(128)(4,1)S(1)}, pred[96]{0:T(512)(128)(4,1)}, u32[]{:S(2)}) copy-start(pred[96]{0:T(512)(128)(4,1)} %compare_and_fusion) | copy-start | bytes 292
  138.8 12.6 %copy-start.11 = (pred[384]{0:T(512)(128)(4,1)S(1)}, pred[384]{0:T(512)(128)(4,1)}, u32[]{:S(2)}) copy-start(pred[384]{0:T(512)(128)(4,1)} %fusion.21) | copy-start | bytes 1156
  138.8 12.0 %all-to-all-start.1 = ((bf16[4,96,436]{2,1,0:T(8,128)(2,1)}), bf16[4,96,436]{2,1,0:T(8,128)(2,1)S(1)}, u32[]{:S(2)}, u32[]{:S(2)}) async-start(bf16[4,96,436]{2,1,0:T(8,128)(2,1)} %gather_fusion), calls=%async_computation.1 | async-start | bytes 786432 | tf_op jit(solution)/shard_map/all_to_all | solution.py:163

commit v3 on v2

v3 whole, which is shorter than its diff:
```python
import functools

import jax
import jax.numpy as jnp
from jax import lax
from jax.experimental import pallas as pl
from jax.experimental.pallas import tpu as pltpu
from jax.sharding import Mesh
from jax.sharding import PartitionSpec as P

D = 5120
RANK = 4
MEMBER_TOKENS = 16
POPULATION = 192
MEMBER = ("z", "x", "lo")
TENSOR = ("hi", "core")
SIGMA = 0.25 * D**-0.5
MIXING = SIGMA * RANK**-0.5
GRADIENT_SCALE = 1.0 / (POPULATION * SIGMA * RANK**0.5)


def shifted(array, axis, step):
    size = lax.axis_size(axis)
    return lax.ppermute(array, axis, [(k, (k + step) % size) for k in range(size)])


def gathered(array, axes):
    copies = jnp.broadcast_to(array, (lax.axis_size(axes), *array.shape))
    return lax.all_to_all(copies, axes, split_axis=0, concat_axis=0, tiled=True)


def wrapped(stack, start, sign=1):
    count = stack.shape[0]
    order = (start + sign * jnp.arange(count)) % count
    return jnp.take(stack, order, axis=0, mode="clip")


def dot_t(a, b):
    return lax.dot_general(a, b, (((1,), (1,)), ((), ())), preferred_element_type=jnp.float32)


CHUNK = 256


def partial_kernel(rows, factors, where_ref, near_ref, weight_ref, sent_ref, kept_ref, token_ref, left_ref):
    slot = near_ref.shape[1] // 2
    block = 2 * rows
    n_hi = sent_ref.shape[0]
    wide, features = weight_ref.shape
    for side in range(2):
        for j in range(n_hi):
            z = 2 * ((where_ref[0] + j) % n_hi) + (where_ref[1] if side else 1 - where_ref[1])
            at = (side * n_hi + j) * block
            token_ref[at : at + rows] = near_ref[z, :rows]
            token_ref[at + rows : at + block] = near_ref[z, slot : slot + rows]
            left_ref[side * n_hi + j] = near_ref[z]
    row = lax.broadcasted_iota(jnp.int32, (block, 2 * slot), 0)
    col = lax.broadcasted_iota(jnp.int32, (block, 2 * slot), 1)
    place = col % slot - rows
    same = (row // rows == col // slot) & (place >= 0) & (place < factors)
    same &= row % rows // MEMBER_TOKENS == place // RANK
    k = lax.broadcasted_iota(jnp.int32, (2 * slot, CHUNK), 0)
    c = lax.broadcasted_iota(jnp.int32, (2 * slot, CHUNK), 1)
    pick = jnp.where(c == CHUNK - 64 + k % RANK, 1.0, 0.0).astype(jnp.bfloat16)
    for n in range(0, wide, CHUNK):
        for side, out_ref in enumerate((sent_ref, kept_ref)):
            some = token_ref[side * n_hi * block : (side + 1) * n_hi * block]
            product = dot_t(some, weight_ref[n : n + CHUNK]).reshape(n_hi, block, CHUNK)
            if n + CHUNK < wide:
                out_ref[:, :, n : n + CHUNK] = product.astype(out_ref.dtype)
                continue
            for j in range(n_hi):
                projection = dot_t(some[j * block : (j + 1) * block], left_ref[side * n_hi + j])
                projection = jnp.where(same, projection, 0.0).astype(jnp.bfloat16)
                tail = jnp.dot(projection, pick, preferred_element_type=jnp.float32)
                out_ref[j, :, n : n + CHUNK] = (product[j] + tail).astype(out_ref.dtype)


def partials(near, weights, where, rows, factors):
    n_hi = 4
    wide, features = weights.shape
    blocks = near.reshape(2 * n_hi, -1, features)
    block = 2 * rows
    vmem = pl.BlockSpec(memory_space=pltpu.VMEM)
    half = jax.ShapeDtypeStruct((n_hi, block, wide), jnp.bfloat16)
    return pl.pallas_call(
        functools.partial(partial_kernel, rows, factors),
        in_specs=[pl.BlockSpec(memory_space=pltpu.SMEM), vmem, vmem],
        out_specs=[vmem, vmem],
        out_shape=[half, half],
        scratch_shapes=[
            pltpu.VMEM((2 * n_hi * block, features), jnp.bfloat16),
            pltpu.VMEM((2 * n_hi, *blocks.shape[1:]), jnp.bfloat16),
        ],
        cost_estimate=pl.CostEstimate(
            flops=4 * n_hi * block * wide * features,
            transcendentals=0,
            bytes_accessed=2 * (wide * features + blocks.size + 2 * n_hi * block * wide),
        ),
    )(where, blocks, weights)


def body(tokens, up_weight, left_factors, right_factors, fitness):
    f32, bf16 = jnp.float32, jnp.bfloat16
    hi, core, x = lax.axis_index("hi"), lax.axis_index("core"), lax.axis_index("x")
    rows, features = tokens.shape
    factors = left_factors.shape[0]
    columns = up_weight.shape[1]
    own = right_factors.shape[0]
    n_x, n_hi, n_z, n_lo = (lax.axis_size(a) for a in ("x", "hi", "z", "lo"))
    wide = -(-(n_x * columns + RANK) // 128) * 128

    weight = up_weight.T
    weight_after = shifted(weight, "x", -1)
    weight_before = shifted(weight, "x", 1)
    mine = jnp.concatenate([tokens, left_factors, jnp.zeros((4, features), bf16)], 0)
    near = gathered(mine, ("z", "lo"))
    weight_far = shifted(weight, "x", 2)
    right_after = shifted(right_factors, "hi", -1)
    right_before = shifted(right_factors, "hi", 1)
    right_far = shifted(right_factors, "hi", 2)
    right_same = jnp.stack([right_factors, right_after, right_far, right_before])
    near, right_same = lax.optimization_barrier((near, right_same))
    near_left = near[:, rows : rows + factors]
    weights = jnp.concatenate(
        [weight, weight_after, weight_far, weight_before, jnp.zeros((wide - n_x * columns, features), bf16)], 0
    )

    block = n_lo * rows
    sent, kept = partials(near, weights, jnp.stack([hi, core]), rows, factors)
    other = shifted(sent, "core", 1)

    def both(j, start, stop):
        return kept[j, start:stop].astype(f32) + other[j, start:stop].astype(f32)

    cut = block // 2
    far_after = shifted(both(2, 0, cut).astype(bf16), "hi", 1)
    far_before = shifted(both(2, cut, block).astype(bf16), "hi", -1)
    high_before = shifted(both(1, cut, block).astype(bf16), "hi", 1)
    low_after = shifted(both(3, 0, cut).astype(bf16), "hi", -1)
    low_before = shifted((both(1, 0, cut) + far_after.astype(f32)).astype(bf16), "hi", 1)
    high_after = shifted((both(3, cut, block) + far_before.astype(f32)).astype(bf16), "hi", -1)
    low = both(0, 0, cut) + low_before.astype(f32) + low_after.astype(f32)
    high = both(0, cut, block) + high_before.astype(f32) + high_after.astype(f32)
    total = jnp.concatenate([low, high], 0).astype(bf16)

    tail = total[:, n_x * columns : n_x * columns + RANK]
    pieces = [jnp.concatenate([total[:, j * columns : (j + 1) * columns], tail], 1) for j in range(n_x)]
    pieces = wrapped(jnp.stack(pieces), n_x - x)
    whole = lax.all_to_all(pieces, "x", split_axis=0, concat_axis=0, tiled=True)
    whole = whole.reshape(n_x * block, columns + RANK)
    row = lax.broadcasted_iota(jnp.int32, (n_x * block, own), 0)
    col = lax.broadcasted_iota(jnp.int32, (n_x * block, own), 1)
    tiled = jnp.tile(whole[:, columns:], (1, own // RANK))
    spread = jnp.where(row // MEMBER_TOKENS == col // RANK, tiled, 0)
    correction = jnp.dot(spread, right_factors, preferred_element_type=f32)
    hidden = (whole[:, :columns].astype(f32) + MIXING * correction).astype(bf16)

    left_all = gathered(near_left, "x")
    left_all = left_all.reshape(n_x, n_z, n_lo * factors, features).transpose(1, 0, 2, 3)
    left_all = left_all.reshape(-1, features)
    fit = jnp.repeat(fitness, RANK)
    weighted = (fit[:, None] * left_all.astype(f32)).astype(bf16)
    right_other = shifted(right_same, "core", 1)
    here = core == 0
    right_all = jnp.stack([jnp.where(here, right_same, right_other), jnp.where(here, right_other, right_same)], 1)
    right_all = wrapped(right_all, n_hi - hi).reshape(-1, columns)
    gradient = jnp.einsum("kd,kf->df", weighted, right_all, preferred_element_type=f32)
    return hidden, (gradient * GRADIENT_SCALE).astype(bf16)


def solution(mesh):
    finer = Mesh(mesh.devices.reshape(8, 4, 2, 4, 2), MEMBER + TENSOR)
    return jax.shard_map(
        body,
        mesh=finer,
        in_specs=(P(MEMBER, TENSOR), P(TENSOR, MEMBER), P(MEMBER, TENSOR), P(TENSOR, MEMBER), P()),
        out_specs=(P(TENSOR, MEMBER), P(TENSOR, MEMBER)),
        check_vma=False,
    )
```

time: 154 us -> 135 us (0.88)
  the two profiles are of different devices: /device:TPU:136 before, /device:TPU:56 now
where the time goes in v3:
time: 135 us; the launch traced here: 134 us
  starting transfers between devices  75.9 us (56%)
  waiting for transfers between devices  21 us (16%)
  local copies, waits for them, and re-layouts  15 us (11%)
  other arithmetic  11.8 us (9%)
  Pallas kernels  6.27 us (5%)
  matrix products  2.61 us (2%)
    ppermute x14, starting transfers between devices, shifted(): lax.ppermute(array, axis, [(k, (k + step) % size) for k in range(size)])  52.8 us
    all_to_all x2, starting transfers between devices, gathered(): return lax.all_to_all(copies, axes, split_axis=0, concat_axis=0, tiled=True)  16.1 us
    ppermute x14, waiting for transfers between devices, shifted(): lax.ppermute(array, axis, [(k, (k + step) % size) for k in range(size)])  14.2 us
    all_to_all x1, starting transfers between devices, body(): whole = lax.all_to_all(pieces, 'x', split_axis=0, concat_axis=0, tiled=True)  7.04 us
    pallas_call x1, Pallas kernels, partials(): pl.pallas_call(functools.partial(partial_kernel, rows, factors), in_specs...  6.27 us
    unnamed x35, local copies, waits for them, and re-layouts  5.91 us
    all_to_all x1, waiting for transfers between devices, body(): whole = lax.all_to_all(pieces, 'x', split_axis=0, concat_axis=0, tiled=True)  5.8 us
    gather x2, local copies, waits for them, and re-layouts, wrapped(): return jnp.take(stack, order, axis=0, mode='clip')  2.79 us
  transfers between devices with their start and end apart: 17, of which 6 were waited for; matrix products, arithmetic and copies ran while one was open for 14% of the time, Pallas kernels for 0%

profile of v3, /device:TPU:56, one launch (start us, length us, event | category | flops | bytes accessed | tf_op | source)
XLA Modules:
  0.0 133.6 jit_solution(17682439357304406043)
XLA Ops:
  0.7 0.9 maximum_maximum_fusion
  1.7 1.2 broadcast_in_dim.28
  2.9 11.8 %all-to-all-start = ((bf16[16,64,640]{2,1,0:T(8,128)(2,1)}), bf16[16,64,640]{2,1,0:T(8,128)(2,1)S(1)}, u32[]{:S(2)}, u32[]{:S(2)}) async-start(bf16[16,64,640]{2,1,0:T(8,128)(2,1)} %broadcast_in_dim.28), calls=%async_computation | async-start | bytes 2621440 | tf_op jit(solution)/shard_map/all_to_all | solution.py:29
  14.7 4.7 %collective-permute-start.3 = (bf16[432,640]{1,0:T(8,128)(2,1)S(1)}, bf16[432,640]{1,0:T(8,128)(2,1)}, u32[]{:S(2)}, u32[]{:S(2)}) collective-permute-start(bf16[432,640]{1,0:T(8,128)(2,1)S(1)} %bitcast.72), channel_id=1, source_target_pairs={{0,48},{16,0},{32,16},{48,32},{1,49},{17,1},{33,17},{49,33},{2,50}... | collective-permute-start | bytes 1658888 | tf_op jit(solution)/shard_map/ppermute | solution.py:24
  19.4 2.7 %collective-permute-start.4 = (bf16[432,640]{1,0:T(8,128)(2,1)S(1)}, bf16[432,640]{1,0:T(8,128)(2,1)S(1)}, u32[]{:S(2)}, u32[]{:S(2)}) collective-permute-start(bf16[432,640]{1,0:T(8,128)(2,1)S(1)} %bitcast.73), channel_id=1, source_target_pairs={{0,32},{16,48},{32,0},{48,16},{1,33},{17,49},{33,1},{49,17},{2,34}... | collective-permute-start | bytes 1658888 | tf_op jit(solution)/shard_map/ppermute | solution.py:24
  22.1 2.8 %collective-permute-start.5 = (bf16[432,640]{1,0:T(8,128)(2,1)S(1)}, bf16[432,640]{1,0:T(8,128)(2,1)S(1)}, u32[]{:S(2)}, u32[]{:S(2)}) collective-permute-start(bf16[432,640]{1,0:T(8,128)(2,1)S(1)} %bitcast.74), channel_id=1, source_target_pairs={{0,16},{16,32},{32,48},{48,0},{1,17},{17,33},{33,49},{49,1},{2,18}... | collective-permute-start | bytes 1658888 | tf_op jit(solution)/shard_map/ppermute | solution.py:24
  24.9 4.0 %collective-permute-start = (bf16[96,432]{1,0:T(8,128)(2,1)S(1)}, bf16[96,432]{1,0:T(8,128)(2,1)S(1)}, u32[]{:S(2)}, u32[]{:S(2)}) collective-permute-start(bf16[96,432]{1,0:T(8,128)(2,1)S(1)} %copy-done.6), channel_id=1, source_target_pairs={{0,6},{2,0},{4,2},{6,4},{1,7},{3,1},{5,3},{7,5},{8,14},{10,8},{12,... | collective-permute-start | bytes 248840 | tf_op jit(solution)/shard_map/ppermute | solution.py:24
  29.0 2.9 %collective-permute-start.1 = (bf16[96,432]{1,0:T(8,128)(2,1)S(1)}, bf16[96,432]{1,0:T(8,128)(2,1)S(1)}, u32[]{:S(2)}, u32[]{:S(2)}) collective-permute-start(bf16[96,432]{1,0:T(8,128)(2,1)S(1)} %copy-done.6), channel_id=1, source_target_pairs={{0,4},{2,6},{4,0},{6,2},{1,5},{3,7},{5,1},{7,3},{8,12},{10,14},{12... | collective-permute-start | bytes 248840 | tf_op jit(solution)/shard_map/ppermute | solution.py:24
  31.9 0.8 constant_dynamic-update-slice_fusion.3
  32.7 8.4 %collective-permute-done = bf16[96,432]{1,0:T(8,128)(2,1)S(1)} collective-permute-done((bf16[96,432]{1,0:T(8,128)(2,1)S(1)}, bf16[96,432]{1,0:T(8,128)(2,1)S(1)}, u32[]{:S(2)}, u32[]{:S(2)}) %collective-permute-start) | collective-permute-done | bytes 82976 | tf_op jit(solution)/shard_map/ppermute | solution.py:24
  41.2 4.0 %collective-permute-start.2 = (bf16[96,432]{1,0:T(8,128)(2,1)S(1)}, bf16[96,432]{1,0:T(8,128)(2,1)S(1)}, u32[]{:S(2)}, u32[]{:S(2)}) collective-permute-start(bf16[96,432]{1,0:T(8,128)(2,1)S(1)} %copy-done.6), channel_id=1, source_target_pairs={{0,2},{2,4},{4,6},{6,0},{1,3},{3,5},{5,7},{7,1},{8,10},{10,12},{12... | collective-permute-start | bytes 248840 | tf_op jit(solution)/shard_map/ppermute | solution.py:24
  45.2 0.6 pad_add_fusion.where_ref
  45.8 2.9 %collective-permute-done.2 = bf16[96,432]{1,0:T(8,128)(2,1)S(1)} collective-permute-done((bf16[96,432]{1,0:T(8,128)(2,1)S(1)}, bf16[96,432]{1,0:T(8,128)(2,1)S(1)}, u32[]{:S(2)}, u32[]{:S(2)}) %collective-permute-start.2) | collective-permute-done | bytes 82976 | tf_op jit(solution)/shard_map/ppermute | solution.py:24
  48.7 1.0 pad_maximum_fusion.1
  49.7 1.9 %constant_dynamic-update-slice_fusion.2 = bf16[1792,640]{1,0:T(8,128)(2,1)} fusion(bf16[1792,640]{1,0:T(8,128)(2,1)} %constant_dynamic-update-slice_fusion.3, bf16[432,640]{1,0:T(8,128)(2,1)} %collective-permute-done.3), kind=kLoop, calls=%fused_computation.64 | loop fusion | bytes 1105920
  51.7 0.9 constant_dynamic-update-slice_fusion.1
  52.6 0.9 constant_dynamic-update-slice_fusion
  53.4 0.6 broadcast_dynamic-update-slice_fusion.weight_ref
  54.1 1.1 copy-done
  55.2 6.3 %shard_map.68 = (bf16[4,96,1792]{2,1,0:T(8,128)(2,1)}, bf16[4,96,1792]{2,1,0:T(8,128)(2,1)}) custom-call(s32[2]{0:T(128)} %pad_add_fusion.where_ref, bf16[8,128,640]{2,1,0:T(8,128)(2,1)} %bitcast.67, bf16[1792,640]{1,0:T(8,128)(2,1)} %broadcast_dynamic-update-slice_fusion.weight_ref), custom_call_target="tpu_custom_call" | custom-call | flops 1761607680 | bytes 6356992 | tf_op jit(solution)/shard_map/pallas_call | solution.py:86
  61.4 1.9 %collective-permute-start.6 = (bf16[4,96,1792]{2,1,0:T(8,128)(2,1)}, bf16[4,96,1792]{2,1,0:T(8,128)(2,1)S(1)}, u32[]{:S(2)}, u32[]{:S(2)}) collective-permute-start(bf16[4,96,1792]{2,1,0:T(8,128)(2,1)} %get-tuple-element.8), channel_id=1, source_target_pairs={{0,1},{1,0},{2,3},{3,2},{4,5},{5,4},{6,7},{7,6},{8,9},{9,8},{10,11... | collective-permute-start | bytes 4128776 | tf_op jit(solution)/shard_map/ppermute | solution.py:24
  63.6 0.8 copy.26
  64.5 0.6 compare_and_fusion
  65.6 0.6 iota_shift-right-logical_fusion.1
  66.1 0.5 collective-permute-done.6
  66.7 2.6 %fusion.9 = (bf16[48,1792]{1,0:T(8,128)(2,1)S(1)}, bf16[48,1792]{1,0:T(8,128)(2,1)}, bf16[48,1792]{1,0:T(8,128)(2,1)}, bf16[48,1792]{1,0:T(8,128)(2,1)}) fusion(bf16[4,96,1792]{2,1,0:T(8,128)(2,1)S(1)} %collective-permute-done.6, bf16[4,96,1792]{2,1,0:T(8,128)(2,1)} %get-tuple-element.7), kind=kLoop, calls=%fused_computation.35 | loop fusion | flops 1376256 | bytes 2064384 | tf_op jit(solution)/shard_map/convert_element_type | solution.py:137
  69.2 5.1 %collective-permute-start.7 = (bf16[48,1792]{1,0:T(8,128)(2,1)S(1)}, bf16[48,1792]{1,0:T(8,128)(2,1)S(1)}, u32[]{:S(2)}, u32[]{:S(2)}) collective-permute-start(bf16[48,1792]{1,0:T(8,128)(2,1)S(1)} %get-tuple-element.12), channel_id=1, source_target_pairs={{0,2},{2,4},{4,6},{6,0},{1,3},{3,5},{5,7},{7,1},{8,10},{10,12},{12... | collective-permute-start | bytes 516104 | tf_op jit(solution)/shard_map/ppermute | solution.py:24
  74.4 1.0 slice.93
  75.4 2.1 %collective-permute-start.13 = (bf16[4,96,432]{2,1,0:T(8,128)(2,1)S(1)}, bf16[4,96,432]{2,1,0:T(8,128)(2,1)S(1)}, u32[]{:S(2)}, u32[]{:S(2)}) collective-permute-start(bf16[4,96,432]{2,1,0:T(8,128)(2,1)S(1)} %pad_maximum_fusion.1), channel_id=1, source_target_pairs={{0,1},{1,0},{2,3},{3,2},{4,5},{5,4},{6,7},{7,6},{8,9},{9,8},{10,11... | collective-permute-start | bytes 995336 | tf_op jit(solution)/shard_map/ppermute | solution.py:24
  77.5 1.1 broadcast_in_dim.34
  78.6 4.3 %all-to-all-start.2 = ((bf16[4,16,12,640]{3,1,2,0:T(8,128)(2,1)}), bf16[4,16,12,640]{3,1,2,0:T(8,128)(2,1)S(1)}, u32[]{:S(2)}, u32[]{:S(2)}) async-start(bf16[4,16,12,640]{3,1,2,0:T(8,128)(2,1)} %broadcast_in_dim.34), calls=%async_computation.2 | async-start | bytes 1966080 | tf_op jit(solution)/shard_map/all_to_all | solution.py:29
  82.8 2.8 %collective-permute-start.11 = (bf16[48,1792]{1,0:T(8,128)(2,1)}, bf16[48,1792]{1,0:T(8,128)(2,1)}, u32[]{:S(2)}, u32[]{:S(2)}) collective-permute-start(bf16[48,1792]{1,0:T(8,128)(2,1)} %get-tuple-element.13), channel_id=1, source_target_pairs={{0,6},{2,0},{4,2},{6,4},{1,7},{3,1},{5,3},{7,5},{8,14},{10,8},{12,... | collective-permute-start | bytes 516104 | tf_op jit(solution)/shard_map/ppermute | solution.py:24
  85.6 5.9 %collective-permute-start.9 = (bf16[48,1792]{1,0:T(8,128)(2,1)}, bf16[48,1792]{1,0:T(8,128)(2,1)}, u32[]{:S(2)}, u32[]{:S(2)}) collective-permute-start(bf16[48,1792]{1,0:T(8,128)(2,1)} %get-tuple-element.15), channel_id=1, source_target_pairs={{0,6},{2,0},{4,2},{6,4},{1,7},{3,1},{5,3},{7,5},{8,14},{10,8},{12,... | collective-permute-start | bytes 516104 | tf_op jit(solution)/shard_map/ppermute | solution.py:24
  91.5 1.7 %fusion.6 = bf16[48,1792]{1,0:T(8,128)(2,1)} fusion(bf16[48,1792]{1,0:T(8,128)(2,1)S(1)} %collective-permute-done.7, bf16[4,96,1792]{2,1,0:T(8,128)(2,1)} %copy-done.2, bf16[4,96,1792]{2,1,0:T(8,128)(2,1)S(1)} %copy-done.1), kind=kLoop, calls=%fused_computation.27 | loop fusion | flops 516096 | bytes 688128 | tf_op jit(solution)/shard_map/convert_element_type | solution.py:141
  93.2 2.0 %collective-permute-start.8 = (bf16[48,1792]{1,0:T(8,128)(2,1)}, bf16[48,1792]{1,0:T(8,128)(2,1)}, u32[]{:S(2)}, u32[]{:S(2)}) collective-permute-start(bf16[48,1792]{1,0:T(8,128)(2,1)} %fusion.6), channel_id=1, source_target_pairs={{0,2},{2,4},{4,6},{6,0},{1,3},{3,5},{5,7},{7,1},{8,10},{10,12},{12... | collective-permute-start | bytes 516104 | tf_op jit(solution)/shard_map/ppermute | solution.py:24
  95.4 1.5 %gather_fusion.1 = bf16[4,2,96,432]{3,2,1,0:T(8,128)(2,1)} fusion(bf16[4,2,96,432]{3,2,0,1:T(8,128)(2,1)S(1)} %pad_maximum_fusion, s32[1024]{0:T(1024)S(1)} %get-tuple-element.25), kind=kCustom, calls=%fused_computation.1 | custom fusion | bytes 1327120 | tf_op jit(solution)/shard_map/jit(_take)/gather | solution.py:35
  96.9 1.0 all-to-all-done.2
  97.9 0.8 copy.28
  98.7 4.8 %collective-permute-start.10 = (bf16[48,1792]{1,0:T(8,128)(2,1)}, bf16[48,1792]{1,0:T(8,128)(2,1)S(1)}, u32[]{:S(2)}, u32[]{:S(2)}) collective-permute-start(bf16[48,1792]{1,0:T(8,128)(2,1)} %get-tuple-element.14), channel_id=1, source_target_pairs={{0,2},{2,4},{4,6},{6,0},{1,3},{3,5},{5,7},{7,1},{8,10},{10,12},{12... | collective-permute-start | bytes 516104 | tf_op jit(solution)/shard_map/ppermute | solution.py:24
  103.5 1.4 %fusion.8 = (bf16[48,1792]{1,0:T(8,128)(2,1)S(1)}, bf16[48,1792]{1,0:T(8,128)(2,1)S(1)}) fusion(bf16[48,1792]{1,0:T(8,128)(2,1)} %collective-permute-done.9, bf16[48,1792]{1,0:T(8,128)(2,1)} %collective-permute-done.8, bf16[4,96,1792]{2,1,0:T(8,128)(2,1)} %copy-done.2, bf16[4,96,1792]{2,1,0:T(8,128)(2,1)S(1)} %copy-done.1, ...), kind=kLoop, calls=%fused_computation.30 | loop fusion | flops 1204224 | bytes 1548288 | tf_op jit(solution)/shard_map/convert.2
  104.9 7.0 %collective-permute-start.12 = (bf16[48,1792]{1,0:T(8,128)(2,1)S(1)}, bf16[48,1792]{1,0:T(8,128)(2,1)S(1)}, u32[]{:S(2)}, u32[]{:S(2)}) collective-permute-start(bf16[48,1792]{1,0:T(8,128)(2,1)S(1)} %get-tuple-element.11), channel_id=1, source_target_pairs={{0,6},{2,0},{4,2},{6,4},{1,7},{3,1},{5,3},{7,5},{8,14},{10,8},{12,... | collective-permute-start | bytes 516104 | tf_op jit(solution)/shard_map/ppermute | solution.py:24
  112.6 2.3 %collective-permute-done.12 = bf16[48,1792]{1,0:T(8,128)(2,1)S(1)} collective-permute-done((bf16[48,1792]{1,0:T(8,128)(2,1)S(1)}, bf16[48,1792]{1,0:T(8,128)(2,1)S(1)}, u32[]{:S(2)}, u32[]{:S(2)}) %collective-permute-start.12) | collective-permute-done | bytes 172064 | tf_op jit(solution)/shard_map/ppermute | solution.py:24
  114.9 1.0 fusion.5
  116.3 1.3 gather_fusion
  117.6 7.0 %all-to-all-start.1 = ((bf16[4,96,436]{2,1,0:T(8,128)(2,1)}), bf16[4,96,436]{2,1,0:T(8,128)(2,1)S(1)}, u32[]{:S(2)}, u32[]{:S(2)}) async-start(bf16[4,96,436]{2,1,0:T(8,128)(2,1)} %gather_fusion), calls=%async_computation.1 | async-start | bytes 786432 | tf_op jit(solution)/shard_map/all_to_all | solution.py:150
  124.7 1.5 %fusion = bf16[640,432]{0,1:T(8,128)(2,1)} fusion(bf16[768,640]{1,0:T(8,128)(2,1)S(1)} %bitcast.70, bf16[768,432]{1,0:T(8,128)(2,1)S(1)} %bitcast.71), kind=kOutput, calls=%fused_computation.4 | convolution fusion | flops 425226240 | bytes 2199552 | tf_op jit(solution)/shard_map/kd,kf->df/dot_general | solution.py:168
  126.2 5.8 %all-to-all-done.1 = bf16[4,96,436]{2,1,0:T(8,128)(2,1)S(1)} async-done(((bf16[4,96,436]{2,1,0:T(8,128)(2,1)}), bf16[4,96,436]{2,1,0:T(8,128)(2,1)S(1)}, u32[]{:S(2)}, u32[]{:S(2)}) %all-to-all-start.1) | async-done | bytes 334880 | tf_op jit(solution)/shard_map/all_to_all | solution.py:150
  132.6 1.1 fusion.2
  (64 shorter events, 2.6 us)
Async XLA Ops:
  1.6 13.0 %copy-start.4 = (bf16[640,432]{0,1:T(8,128)(2,1)S(1)}, bf16[640,432]{0,1:T(8,128)(2,1)}, u32[]{:S(2)}) copy-start(bf16[640,432]{0,1:T(8,128)(2,1)} %param.6) | copy-start | bytes 1658884
  1.7 23.2 %copy-start.6 = (bf16[96,432]{1,0:T(8,128)(2,1)S(1)}, bf16[96,432]{1,0:T(8,128)(2,1)}, u32[]{:S(2)}) copy-start(bf16[96,432]{1,0:T(8,128)(2,1)} %param.8) | copy-start | bytes 248836
  2.9 51.2 %all-to-all-start = ((bf16[16,64,640]{2,1,0:T(8,128)(2,1)}), bf16[16,64,640]{2,1,0:T(8,128)(2,1)S(1)}, u32[]{:S(2)}, u32[]{:S(2)}) async-start(bf16[16,64,640]{2,1,0:T(8,128)(2,1)} %broadcast_in_dim.28), calls=%async_computation | async-start | bytes 2621440 | tf_op jit(solution)/shard_map/all_to_all | solution.py:29
  14.7 35.0 %collective-permute-start.3 = (bf16[432,640]{1,0:T(8,128)(2,1)S(1)}, bf16[432,640]{1,0:T(8,128)(2,1)}, u32[]{:S(2)}, u32[]{:S(2)}) collective-permute-start(bf16[432,640]{1,0:T(8,128)(2,1)S(1)} %bitcast.72), channel_id=1, source_target_pairs={{0,48},{16,0},{32,16},{48,32},{1,49},{17,1},{33,17},{49,33},{2,50}... | collective-permute-start | bytes 1658888 | tf_op jit(solution)/shard_map/ppermute | solution.py:24
  19.4 32.3 %collective-permute-start.4 = (bf16[432,640]{1,0:T(8,128)(2,1)S(1)}, bf16[432,640]{1,0:T(8,128)(2,1)S(1)}, u32[]{:S(2)}, u32[]{:S(2)}) collective-permute-start(bf16[432,640]{1,0:T(8,128)(2,1)S(1)} %bitcast.73), channel_id=1, source_target_pairs={{0,32},{16,48},{32,0},{48,16},{1,33},{17,49},{33,1},{49,17},{2,34}... | collective-permute-start | bytes 1658888 | tf_op jit(solution)/shard_map/ppermute | solution.py:24
  22.1 30.5 %collective-permute-start.5 = (bf16[432,640]{1,0:T(8,128)(2,1)S(1)}, bf16[432,640]{1,0:T(8,128)(2,1)S(1)}, u32[]{:S(2)}, u32[]{:S(2)}) collective-permute-start(bf16[432,640]{1,0:T(8,128)(2,1)S(1)} %bitcast.74), channel_id=1, source_target_pairs={{0,16},{16,32},{32,48},{48,0},{1,17},{17,33},{33,49},{49,1},{2,18}... | collective-permute-start | bytes 1658888 | tf_op jit(solution)/shard_map/ppermute | solution.py:24
  24.9 16.3 %collective-permute-start = (bf16[96,432]{1,0:T(8,128)(2,1)S(1)}, bf16[96,432]{1,0:T(8,128)(2,1)S(1)}, u32[]{:S(2)}, u32[]{:S(2)}) collective-permute-start(bf16[96,432]{1,0:T(8,128)(2,1)S(1)} %copy-done.6), channel_id=1, source_target_pairs={{0,6},{2,0},{4,2},{6,4},{1,7},{3,1},{5,3},{7,5},{8,14},{10,8},{12,... | collective-permute-start | bytes 248840 | tf_op jit(solution)/shard_map/ppermute | solution.py:24
  29.0 16.9 %collective-permute-start.1 = (bf16[96,432]{1,0:T(8,128)(2,1)S(1)}, bf16[96,432]{1,0:T(8,128)(2,1)S(1)}, u32[]{:S(2)}, u32[]{:S(2)}) collective-permute-start(bf16[96,432]{1,0:T(8,128)(2,1)S(1)} %copy-done.6), channel_id=1, source_target_pairs={{0,4},{2,6},{4,0},{6,2},{1,5},{3,7},{5,1},{7,3},{8,12},{10,14},{12... | collective-permute-start | bytes 248840 | tf_op jit(solution)/shard_map/ppermute | solution.py:24
  41.2 7.6 %copy-start.8 = (bf16[96,432]{1,0:T(8,128)(2,1)}, bf16[96,432]{1,0:T(8,128)(2,1)S(1)}, u32[]{:S(2)}) copy-start(bf16[96,432]{1,0:T(8,128)(2,1)S(1)} %collective-permute-done) | copy-start | bytes 248836
  41.2 7.6 %collective-permute-start.2 = (bf16[96,432]{1,0:T(8,128)(2,1)S(1)}, bf16[96,432]{1,0:T(8,128)(2,1)S(1)}, u32[]{:S(2)}, u32[]{:S(2)}) collective-permute-start(bf16[96,432]{1,0:T(8,128)(2,1)S(1)} %copy-done.6), channel_id=1, source_target_pairs={{0,2},{2,4},{4,6},{6,0},{1,3},{3,5},{5,7},{7,1},{8,10},{10,12},{12... | collective-permute-start | bytes 248840 | tf_op jit(solution)/shard_map/ppermute | solution.py:24
  45.8 2.9 %copy-start.9 = (bf16[96,432]{1,0:T(8,128)(2,1)}, bf16[96,432]{1,0:T(8,128)(2,1)S(1)}, u32[]{:S(2)}) copy-start(bf16[96,432]{1,0:T(8,128)(2,1)S(1)} %collective-permute-done.1) | copy-start | bytes 248836
  54.1 1.1 copy-start
  55.2 8.2 %copy-start.10 = (f32[192]{0:T(256)S(1)}, f32[192]{0:T(256)}, u32[]{:S(2)}) copy-start(f32[192]{0:T(256)} %param.9) | copy-start | bytes 2308
  61.4 5.2 %collective-permute-start.6 = (bf16[4,96,1792]{2,1,0:T(8,128)(2,1)}, bf16[4,96,1792]{2,1,0:T(8,128)(2,1)S(1)}, u32[]{:S(2)}, u32[]{:S(2)}) collective-permute-start(bf16[4,96,1792]{2,1,0:T(8,128)(2,1)} %get-tuple-element.8), channel_id=1, source_target_pairs={{0,1},{1,0},{2,3},{3,2},{4,5},{5,4},{6,7},{7,6},{8,9},{9,8},{10,11... | collective-permute-start | bytes 4128776 | tf_op jit(solution)/shard_map/ppermute | solution.py:24
  66.7 7.7 %copy-start.2 = (bf16[4,96,1792]{2,1,0:T(8,128)(2,1)}, bf16[4,96,1792]{2,1,0:T(8,128)(2,1)S(1)}, u32[]{:S(2)}) copy-start(bf16[4,96,1792]{2,1,0:T(8,128)(2,1)S(1)} %collective-permute-done.6) | copy-start | bytes 4128772
  69.2 22.3 %collective-permute-start.7 = (bf16[48,1792]{1,0:T(8,128)(2,1)S(1)}, bf16[48,1792]{1,0:T(8,128)(2,1)S(1)}, u32[]{:S(2)}, u32[]{:S(2)}) collective-permute-start(bf16[48,1792]{1,0:T(8,128)(2,1)S(1)} %get-tuple-element.12), channel_id=1, source_target_pairs={{0,2},{2,4},{4,6},{6,0},{1,3},{3,5},{5,7},{7,1},{8,10},{10,12},{12... | collective-permute-start | bytes 516104 | tf_op jit(solution)/shard_map/ppermute | solution.py:24
  75.4 16.2 %copy-start.1 = (bf16[4,96,1792]{2,1,0:T(8,128)(2,1)S(1)}, bf16[4,96,1792]{2,1,0:T(8,128)(2,1)}, u32[]{:S(2)}) copy-start(bf16[4,96,1792]{2,1,0:T(8,128)(2,1)} %get-tuple-element.7) | copy-start | bytes 4128772
  75.4 19.9 %collective-permute-start.13 = (bf16[4,96,432]{2,1,0:T(8,128)(2,1)S(1)}, bf16[4,96,432]{2,1,0:T(8,128)(2,1)S(1)}, u32[]{:S(2)}, u32[]{:S(2)}) collective-permute-start(bf16[4,96,432]{2,1,0:T(8,128)(2,1)S(1)} %pad_maximum_fusion.1), channel_id=1, source_target_pairs={{0,1},{1,0},{2,3},{3,2},{4,5},{5,4},{6,7},{7,6},{8,9},{9,8},{10,11... | collective-permute-start | bytes 995336 | tf_op jit(solution)/shard_map/ppermute | solution.py:24
  78.6 19.3 %all-to-all-start.2 = ((bf16[4,16,12,640]{3,1,2,0:T(8,128)(2,1)}), bf16[4,16,12,640]{3,1,2,0:T(8,128)(2,1)S(1)}, u32[]{:S(2)}, u32[]{:S(2)}) async-start(bf16[4,16,12,640]{3,1,2,0:T(8,128)(2,1)} %broadcast_in_dim.34), calls=%async_computation.2 | async-start | bytes 1966080 | tf_op jit(solution)/shard_map/all_to_all | solution.py:29
  82.8 20.6 %collective-permute-start.11 = (bf16[48,1792]{1,0:T(8,128)(2,1)}, bf16[48,1792]{1,0:T(8,128)(2,1)}, u32[]{:S(2)}, u32[]{:S(2)}) collective-permute-start(bf16[48,1792]{1,0:T(8,128)(2,1)} %get-tuple-element.13), channel_id=1, source_target_pairs={{0,6},{2,0},{4,2},{6,4},{1,7},{3,1},{5,3},{7,5},{8,14},{10,8},{12,... | collective-permute-start | bytes 516104 | tf_op jit(solution)/shard_map/ppermute | solution.py:24
  85.6 17.9 %collective-permute-start.9 = (bf16[48,1792]{1,0:T(8,128)(2,1)}, bf16[48,1792]{1,0:T(8,128)(2,1)}, u32[]{:S(2)}, u32[]{:S(2)}) collective-permute-start(bf16[48,1792]{1,0:T(8,128)(2,1)} %get-tuple-element.15), channel_id=1, source_target_pairs={{0,6},{2,0},{4,2},{6,4},{1,7},{3,1},{5,3},{7,5},{8,14},{10,8},{12,... | collective-permute-start | bytes 516104 | tf_op jit(solution)/shard_map/ppermute | solution.py:24
  93.2 10.3 %collective-permute-start.8 = (bf16[48,1792]{1,0:T(8,128)(2,1)}, bf16[48,1792]{1,0:T(8,128)(2,1)}, u32[]{:S(2)}, u32[]{:S(2)}) collective-permute-start(bf16[48,1792]{1,0:T(8,128)(2,1)} %fusion.6), channel_id=1, source_target_pairs={{0,2},{2,4},{4,6},{6,0},{1,3},{3,5},{5,7},{7,1},{8,10},{10,12},{12... | collective-permute-start | bytes 516104 | tf_op jit(solution)/shard_map/ppermute | solution.py:24
  96.9 15.1 %copy-start.5 = (f32[8,4,24]{1,2,0:T(8,128)S(1)}, f32[8,4,24]{1,2,0:T(8,128)}, u32[]{:S(2)}) copy-start(f32[8,4,24]{1,2,0:T(8,128)} %copy.26) | copy-start | bytes 9220
  98.7 13.9 %collective-permute-start.10 = (bf16[48,1792]{1,0:T(8,128)(2,1)}, bf16[48,1792]{1,0:T(8,128)(2,1)S(1)}, u32[]{:S(2)}, u32[]{:S(2)}) collective-permute-start(bf16[48,1792]{1,0:T(8,128)(2,1)} %get-tuple-element.14), channel_id=1, source_target_pairs={{0,2},{2,4},{4,6},{6,0},{1,3},{3,5},{5,7},{7,1},{8,10},{10,12},{12... | collective-permute-start | bytes 516104 | tf_op jit(solution)/shard_map/ppermute | solution.py:24
  104.9 9.9 %collective-permute-start.12 = (bf16[48,1792]{1,0:T(8,128)(2,1)S(1)}, bf16[48,1792]{1,0:T(8,128)(2,1)S(1)}, u32[]{:S(2)}, u32[]{:S(2)}) collective-permute-start(bf16[48,1792]{1,0:T(8,128)(2,1)S(1)} %get-tuple-element.11), channel_id=1, source_target_pairs={{0,6},{2,0},{4,2},{6,4},{1,7},{3,1},{5,3},{7,5},{8,14},{10,8},{12,... | collective-permute-start | bytes 516104 | tf_op jit(solution)/shard_map/ppermute | solution.py:24
  116.0 8.6 %copy-start.3 = (bf16[4,2,96,432]{3,2,1,0:T(8,128)(2,1)S(1)}, bf16[4,2,96,432]{3,2,1,0:T(8,128)(2,1)}, u32[]{:S(2)}) copy-start(bf16[4,2,96,432]{3,2,1,0:T(8,128)(2,1)} %gather_fusion.1) | copy-start | bytes 1990660
  117.6 14.4 %all-to-all-start.1 = ((bf16[4,96,436]{2,1,0:T(8,128)(2,1)}), bf16[4,96,436]{2,1,0:T(8,128)(2,1)S(1)}, u32[]{:S(2)}, u32[]{:S(2)}) async-start(bf16[4,96,436]{2,1,0:T(8,128)(2,1)} %gather_fusion), calls=%async_computation.1 | async-start | bytes 786432 | tf_op jit(solution)/shard_map/all_to_all | solution.py:150
  124.6 7.9 %copy-start.7 = (bf16[96,432]{1,0:T(8,128)(2,1)S(1)}, bf16[96,432]{1,0:T(8,128)(2,1)}, u32[]{:S(2)}) copy-start(bf16[96,432]{1,0:T(8,128)(2,1)} %param.8) | copy-start | bytes 248836
  124.6 7.9 %copy-start.11 = (s32[96]{0:T(128)S(1)}, s32[96]{0:T(128)}, u32[]{:S(2)}) copy-start(s32[96]{0:T(128)} %get-tuple-element.29) | copy-start | bytes 1156
  124.6 7.9 %copy-start.12 = (s32[96]{0:T(128)S(1)}, s32[96]{0:T(128)}, u32[]{:S(2)}) copy-start(s32[96]{0:T(128)} %get-tuple-element.30) | copy-start | bytes 1156
  124.7 7.9 %copy-start.13 = (pred[96]{0:T(512)(128)(4,1)S(1)}, pred[96]{0:T(512)(128)(4,1)}, u32[]{:S(2)}) copy-start(pred[96]{0:T(512)(128)(4,1)} %compare_and_fusion) | copy-start | bytes 292
  124.7 7.9 %copy-start.14 = (pred[384]{0:T(512)(128)(4,1)S(1)}, pred[384]{0:T(512)(128)(4,1)}, u32[]{:S(2)}) copy-start(pred[384]{0:T(512)(128)(4,1)} %fusion.32) | copy-start | bytes 1156
